TPU v7x, 256 devices: a whole 4x4x8 slice. The times are simulated.
256 devices in a mesh: prow: 16 (over z, core), pcol: 16 (over y, x).
Axes of the slice: x: 4, y: 4, z: 8, core: 2. Of those that a mesh axis runs over, the one named last changes fastest.
Arguments:
- matrix: float32 [16384, 24576], P('prow', 'pcol'), may hold values from -14 to 142, as said below
Outputs:
- factored: float32 [16384, 24576], P('prow', 'pcol')
- tfactors: float32 [2, 128, 128], replicated
Inputs may be any that keep to these rules, and one draw needn't show every extreme that they name: `matrix`: real entries.
All inputs are finite; a program needn't handle non-finite values.
Results may differ from a plain program's by a relative error of at most 0.0003.
Values sent between devices are 32-bit elements; how exact they have to be, the bound alone decides.
No kernel may reach another device: no remote copies, remote signals or barrier semaphores. Data moves between devices by JAX's collectives and lax.ppermute only.
A program may use at most 128 MiB of HBM per device.

v0:
```python
import jax
import jax.numpy as jnp
from jax import lax
from jax.experimental import pallas as pl
from jax.experimental.pallas import tpu as pltpu
from jax.sharding import PartitionSpec as P


NB = 128
WIDE = 2 * NB
STRIP = 8
LEVELS, CORES = 8, 2

f32, bf16 = jnp.float32, jnp.bfloat16


def three_parts(value):
    first = value.astype(bf16).astype(f32)
    rest = value - first
    second = rest.astype(bf16).astype(f32)
    return first, second, (rest - second).astype(bf16).astype(f32)


def strip_product(left, right):
    a, b, c = three_parts(left)
    d, e, f = three_parts(right)
    return lax.dot_general(
        jnp.concatenate([a, a, b, b, a, c], axis=0).astype(bf16),
        jnp.concatenate([d, e, d, e, f, d], axis=0).astype(bf16),
        (((0,), (0,)), ((), ())),
        preferred_element_type=f32,
    )


def strip_columns(rows, first, lanes):
    return [
        jnp.sum(jnp.where(lanes == first + c, rows, 0.0), axis=1, keepdims=True)
        for c in range(STRIP)
    ]


def identity_matrix():
    rows = lax.broadcasted_iota(jnp.int32, (WIDE, WIDE), 0)
    return (rows == lax.broadcasted_iota(jnp.int32, (WIDE, WIDE), 1)).astype(f32)


def strips_of(half):
    count = WIDE // STRIP // 2
    return half * count, (half + 1) * count


def cholesky_kernel(gram_ref, upper_ref, inverse_ref, work):
    work[:, :WIDE] = gram_ref[...]
    work[:, WIDE:] = identity_matrix()
    lanes = lax.broadcasted_iota(jnp.int32, (STRIP, WIDE), 1)
    row_ids = lax.broadcasted_iota(jnp.int32, (STRIP, WIDE), 0)
    sub_narrow = lax.broadcasted_iota(jnp.int32, (STRIP, 1), 0)
    sub_wide = lax.broadcasted_iota(jnp.int32, (STRIP, 2 * WIDE), 0)
    for half in range(2):
        low, high = half * NB, half * NB + 3 * NB

        def strip(index, carry):
            first = pl.multiple_of(index * STRIP, STRIP)
            rows = work[pl.ds(first, STRIP), :]
            diag = strip_columns(rows[:, :WIDE], first, lanes)
            for c in range(STRIP):
                inverse = lax.rsqrt(diag[c][c : c + 1])
                pivot_row = rows[c : c + 1] * inverse
                factor = jnp.where(sub_narrow > c, diag[c] * inverse, 0.0)
                for d in range(c + 1, STRIP):
                    diag[d] = diag[d] - factor * (diag[d][c : c + 1] * inverse)
                rows = jnp.where(sub_wide == c, pivot_row, rows - factor * pivot_row)
            upper_ref[pl.ds(first, STRIP), :] = jnp.where(
                lanes >= first + row_ids, rows[:, :WIDE], 0.0
            )
            inverse_ref[pl.ds(first, STRIP), :] = rows[:, WIDE:]
            left = jnp.where(lanes >= first + STRIP, rows[:, :WIDE], 0.0)[:, low:]
            work[low:, low:high] = work[low:, low:high] - strip_product(left, rows[:, low:high])
            return carry

        lax.fori_loop(*strips_of(half), strip, 0)


def sharp_product(left, right, right_turned=False):
    a, b, c = three_parts(left)
    d, e, f = three_parts(right)
    axis = 1 if right_turned else 0
    return lax.dot_general(
        jnp.concatenate([a, a, b, b, a, c], axis=1).astype(bf16),
        jnp.concatenate([d, e, d, e, f, d], axis=axis).astype(bf16),
        (((1,), (axis,)), ((), ())),
        preferred_element_type=f32,
    )


def lower_upper_kernel(
    top_ref, r_ref, inverse_ref, square_ref, factors_ref, panel_ref, work, turned_work
):
    total = top_ref[...] + r_ref[...]
    work[:, :WIDE] = total
    work[:, WIDE:] = identity_matrix()
    turned_work[:, :WIDE] = total.T
    turned_work[:, WIDE:] = identity_matrix()
    lanes = lax.broadcasted_iota(jnp.int32, (STRIP, WIDE), 1)
    row_ids = lax.broadcasted_iota(jnp.int32, (STRIP, WIDE), 0)
    sub_narrow = lax.broadcasted_iota(jnp.int32, (STRIP, 1), 0)
    sub_wide = lax.broadcasted_iota(jnp.int32, (STRIP, 2 * WIDE), 0)
    for half in range(2):
        low, high = half * NB, half * NB + 3 * NB

        def strip(index, carry):
            first = pl.multiple_of(index * STRIP, STRIP)
            rows = work[pl.ds(first, STRIP), :]
            turned = turned_work[pl.ds(first, STRIP), :]
            diag = strip_columns(rows[:, :WIDE], first, lanes)
            diag_turned = strip_columns(turned[:, :WIDE], first, lanes)
            for c in range(STRIP):
                inverse = 1.0 / diag[c][c : c + 1]
                factor = jnp.where(sub_narrow > c, diag[c] * inverse, 0.0)
                factor_turned = jnp.where(sub_narrow > c, diag_turned[c], 0.0)
                for d in range(c + 1, STRIP):
                    diag[d] = diag[d] - factor * diag[d][c : c + 1]
                    diag_turned[d] = diag_turned[d] - factor_turned * (
                        diag_turned[d][c : c + 1] * inverse
                    )
                rows = rows - factor * rows[c : c + 1]
                pivot_row = turned[c : c + 1] * inverse
                turned = jnp.where(sub_wide == c, pivot_row, turned - factor_turned * pivot_row)
            after = lanes >= first + STRIP
            left = jnp.where(after, rows[:, :WIDE], 0.0)[:, low:]
            left_turned = jnp.where(after, turned[:, :WIDE], 0.0)[:, low:]
            work[low:, low:high] = work[low:, low:high] - strip_product(
                left_turned, rows[:, low:high]
            )
            turned_work[low:, low:high] = turned_work[low:, low:high] - strip_product(
                left, turned[:, low:high]
            )
            kept = lanes >= first + row_ids
            work[pl.ds(first, STRIP), :WIDE] = jnp.where(kept, rows[:, :WIDE], 0.0)
            work[pl.ds(first, STRIP), WIDE:] = rows[:, WIDE:]
            turned_work[pl.ds(first, STRIP), WIDE:] = turned[:, WIDE:]
            return carry

        lax.fori_loop(*strips_of(half), strip, 0)
    inner = sharp_product(work[:, WIDE:], inverse_ref[...])
    upper_inv = turned_work[:, WIDE:].T
    square_ref[...] = sharp_product(upper_inv, inner)
    panel_ref[...] = -upper_inv
    for k in range(2):
        block = slice(k * NB, (k + 1) * NB)
        factors_ref[k] = sharp_product(work[block, block], inner[block, block], right_turned=True)


square_shape = jax.ShapeDtypeStruct((WIDE, WIDE), f32)


def cholesky(gram):
    return pl.pallas_call(
        cholesky_kernel,
        out_shape=(square_shape,) * 2,
        scratch_shapes=[pltpu.VMEM((WIDE, 2 * WIDE), f32)],
        cost_estimate=pl.CostEstimate(
            flops=14_000_000_000, bytes_accessed=800_000, transcendentals=0
        ),
        name="cholesky",
    )(gram)


def lower_upper(top, r, inverse):
    return pl.pallas_call(
        lower_upper_kernel,
        out_shape=(square_shape, jax.ShapeDtypeStruct((2, NB, NB), f32), square_shape),
        scratch_shapes=[pltpu.VMEM((WIDE, 2 * WIDE), f32)] * 2,
        cost_estimate=pl.CostEstimate(
            flops=17_000_000_000, bytes_accessed=1_600_000, transcendentals=0
        ),
        name="lower_upper",
    )(top, r, inverse)


def product(left, right, precision=lax.Precision.HIGHEST):
    return jnp.dot(left, right, precision=precision, preferred_element_type=f32)


def transposed_product(left, right, precision=lax.Precision.HIGHEST):
    return lax.dot_general(
        left, right, (((0,), (0,)), ((), ())), precision=precision, preferred_element_type=f32
    )


def exchange(pieces, axis, groups=None):
    return lax.all_to_all(pieces, axis, 0, 0, axis_index_groups=groups)


def gather(piece, axis, count, groups=None):
    return exchange(jnp.broadcast_to(piece, (count, *piece.shape)), axis, groups)


def per_device(matrix):
    my_row, my_col = lax.axis_index("prow"), lax.axis_index("pcol")
    rows_count, cols_count = lax.axis_size("prow"), lax.axis_size("pcol")
    core, level = my_row % CORES, my_row // CORES
    on_top, has_panel = my_row == 0, my_col == 0
    levels = [[CORES * z + c for z in range(LEVELS)] for c in range(CORES)]
    rows, cols = matrix.shape
    high = lax.Precision.HIGH

    def permute(value, pairs):
        return lax.ppermute(value, "prow", pairs)

    def swap(value):
        return permute(value, [(i, i ^ 1) for i in range(rows_count)])

    def halves(value):
        low, high = value[: value.shape[0] // CORES], value[value.shape[0] // CORES :]
        return jnp.where(core == 0, low, high), jnp.where(core == 0, high, low)

    column_ids = lax.broadcasted_iota(jnp.int32, (1, cols), 1)
    replaced = has_panel & (column_ids < WIDE)
    pieces, top_rows, source = lax.optimization_barrier(
        (matrix[:, :WIDE].reshape(cols_count, -1, WIDE), matrix[:WIDE], matrix)
    )
    panel_piece = exchange(pieces, "pcol")[0]
    base = jnp.where(replaced, 0.0, source)
    low, high_half = jnp.split(top_rows.T, CORES)
    panel_piece, base = lax.optimization_barrier((panel_piece, base))
    panel = gather(panel_piece, "pcol", cols_count).reshape(rows, WIDE)

    top_half = jnp.where(core == 0, low, permute(high_half, [(0, 1)]))
    held = top_half.reshape(LEVELS, -1, WIDE)
    step = LEVELS // 2
    while step:
        givers = range(0, LEVELS, 2 * step)
        pairs = [(CORES * z + c, CORES * (z + step) + c) for z in givers for c in range(CORES)]
        received = permute(held[step:], pairs)
        held = jnp.where(level % (2 * step) == 0, held[:step], received)
        step //= 2
    panel, top_slice = lax.optimization_barrier((panel, held[0]))

    own_top = jnp.where(on_top, panel[:WIDE], 0.0)
    squares = [transposed_product(panel, panel), own_top]
    squares = jnp.concatenate([a.reshape(rows_count, -1, WIDE) for a in squares], axis=1)
    squares, panel = lax.optimization_barrier((squares, panel))
    square_piece = exchange(squares, "prow")
    mine, other = halves(transposed_product(base, panel, high))
    square_piece = square_piece.sum(0)
    mine = mine + swap(other)
    squares, mine = lax.optimization_barrier((lax.all_gather(square_piece, "prow"), mine))
    gram, top = (a.reshape(WIDE, WIDE) for a in jnp.split(squares, 2, axis=1))
    summed = exchange(mine.reshape(LEVELS, -1, WIDE), "prow", levels).sum(0)
    upper, inverse = cholesky(gram)
    summed = summed + product(top_slice, upper)
    summed = gather(summed, "prow", LEVELS, levels).reshape(-1, WIDE)
    square, factors, panel_weights = lower_upper(top, upper, inverse)
    shifted = jnp.concatenate(
        [jnp.where(on_top, panel[:WIDE] + upper, panel[:WIDE]), panel[WIDE:]], axis=0
    )
    above = jnp.triu(jnp.ones((WIDE, WIDE), jnp.bool_))
    corner = jnp.where(above, -upper - jnp.eye(WIDE, dtype=f32), 0.0)
    corner = jnp.where(on_top & has_panel, corner, base[:WIDE, :WIDE])
    base = base.at[:WIDE, :WIDE].set(corner)
    sibling = swap(summed)
    mine, other = (
        lax.dot_general(
            square, a, (((1,), (1,)), ((), ())), precision=high, preferred_element_type=f32
        )
        for a in (summed, sibling)
    )
    weights = jnp.where(
        core == 0,
        jnp.concatenate([mine, other], axis=1),
        jnp.concatenate([other, mine], axis=1),
    )
    weights = weights.at[:, :WIDE].set(jnp.where(has_panel, panel_weights, weights[:, :WIDE]))
    return (base - product(shifted, weights, high), factors)


def solution(mesh):
    placed = (P("prow", "pcol"),)
    return jax.shard_map(
        per_device, mesh=mesh, in_specs=placed, out_specs=(P("prow", "pcol"), P()), check_vma=False
    )
```

profile of v0, /device:TPU:1, one launch (start us, length us, event | category | flops | bytes accessed | tf_op | source)
XLA Modules:
  0.0 194.0 jit_solution(4928005349071427377)
XLA Ops:
  0.6 2.3 %slice.93 = f32[1024,256]{1,0:T(8,128)} slice(f32[1024,1536]{1,0:T(8,128)} %param.5), slice={[0:1024], [0:256]} | slice | bytes 2097152 | tf_op jit(solution)/shard_map/slice | solution.py:221
  2.9 1.4 slice-done
  4.3 0.5 copy.4
  4.8 0.9 split.17
  5.7 1.3 collective-permute-start
  7.0 7.6 %all-to-all-start = ((f32[16,64,256]{2,1,0:T(8,128)}), f32[16,64,256]{2,1,0:T(8,128)S(1)}, u32[]{:S(2)}, u32[]{:S(2)}) async-start(f32[16,64,256]{2,1,0:T(8,128)} %bitcast), calls=%async_computation | async-start | bytes 2097152 | tf_op jit(solution)/shard_map/all_to_all | solution.py:192
  14.6 1.2 slice_select_fusion
  15.9 0.1 fusion.7
  15.9 9.1 %collective-permute-start.1 = (f32[4,96,256]{2,1,0:T(8,128)S(1)}, f32[4,96,256]{2,1,0:T(8,128)S(1)}, u32[]{:S(2)}, u32[]{:S(2)}) collective-permute-start(f32[4,96,256]{2,1,0:T(8,128)S(1)} %bitcast.40), channel_id=1, source_target_pairs={{0,128},{16,144},{1,129},{17,145},{2,130},{18,146},{3,131},{19,147... | collective-permute-start | bytes 1179656 | tf_op jit(solution)/shard_map/ppermute | solution.py:209
  25.1 6.2 %broadcast_select_fusion = f32[1024,1536]{1,0:T(8,128)} fusion(f32[1024,1536]{1,0:T(8,128)} %param.5, pred[1536]{0:T(1024)(128)(4,1)S(1)} %fusion.5), kind=kLoop, calls=%fused_computation.1 | loop fusion | flops 1572864 | bytes 12584448 | tf_op jit(solution)/shard_map/jit(_where)/select_n | solution.py:224
  31.3 1.1 broadcast_in_dim.30
  32.3 6.6 %all-to-all-start.1 = ((f32[16,64,256]{2,1,0:T(8,128)}), f32[16,64,256]{2,1,0:T(8,128)S(1)}, u32[]{:S(2)}, u32[]{:S(2)}) async-start(f32[16,64,256]{2,1,0:T(8,128)} %broadcast_in_dim.30), calls=%async_computation.1 | async-start | bytes 2097152 | tf_op jit(solution)/shard_map/all_to_all | solution.py:192
  39.0 0.1 broadcast_select_fusion.1
  39.1 2.1 %collective-permute-start.2 = (f32[2,96,256]{2,1,0:T(8,128)S(1)}, f32[2,96,256]{2,1,0:T(8,128)S(1)}, u32[]{:S(2)}, u32[]{:S(2)}) collective-permute-start(f32[2,96,256]{2,1,0:T(8,128)S(1)} %slice.115), channel_id=1, source_target_pairs={{0,64},{16,80},{128,192},{144,208},{1,65},{17,81},{129,193},{145,2... | collective-permute-start | bytes 589832 | tf_op jit(solution)/shard_map/ppermute | solution.py:209
  41.2 2.6 %collective-permute-done.2 = f32[2,96,256]{2,1,0:T(8,128)S(1)} collective-permute-done((f32[2,96,256]{2,1,0:T(8,128)S(1)}, f32[2,96,256]{2,1,0:T(8,128)S(1)}, u32[]{:S(2)}, u32[]{:S(2)}) %collective-permute-start.2) | collective-permute-done | bytes 196640 | tf_op jit(solution)/shard_map/ppermute | solution.py:209
  43.9 1.3 collective-permute-start.3
  45.2 2.2 %collective-permute-done.3 = f32[1,96,256]{2,1,0:T(8,128)S(1)} collective-permute-done((f32[1,96,256]{2,1,0:T(8,128)S(1)}, f32[1,96,256]{2,1,0:T(8,128)S(1)}, u32[]{:S(2)}, u32[]{:S(2)}) %collective-permute-start.3) | collective-permute-done | bytes 98336 | tf_op jit(solution)/shard_map/ppermute | solution.py:209
  47.4 7.9 %all-to-all-done.1 = f32[16,64,256]{2,1,0:T(8,128)S(1)} async-done(((f32[16,64,256]{2,1,0:T(8,128)}), f32[16,64,256]{2,1,0:T(8,128)S(1)}, u32[]{:S(2)}, u32[]{:S(2)}) %all-to-all-start.1) | async-done | bytes 1048608 | tf_op jit(solution)/shard_map/all_to_all | solution.py:192
  55.3 1.8 fusion.9
  57.2 0.9 pad_maximum_fusion
  58.0 7.2 %fusion.10 = f32[1536,256]{1,0:T(8,128)S(1)} fusion(f32[1024,1536]{1,0:T(8,128)} %broadcast_select_fusion, f32[1024,256]{1,0:T(8,128)S(1)} %bitcast.29), kind=kOutput, calls=%fused_computation.31 | convolution fusion | flops 2415919104 | bytes 8912896 | tf_op jit(solution)/shard_map/dot_general | solution.py:186
  65.2 1.0 slice_select_fusion.1
  66.2 2.1 %collective-permute-start.4 = (f32[768,256]{1,0:T(8,128)}, f32[768,256]{1,0:T(8,128)}, u32[]{:S(2)}, u32[]{:S(2)}) collective-permute-start(f32[768,256]{1,0:T(8,128)} %slice_select_fusion.1), channel_id=1, source_target_pairs={{0,16},{16,0},{32,48},{48,32},{64,80},{80,64},{96,112},{112,96},{1... | collective-permute-start | bytes 2359304 | tf_op jit(solution)/shard_map/ppermute | solution.py:209
  68.4 5.7 %all-to-all-start.2 = ((f32[16,32,256]{2,1,0:T(8,128)}), f32[16,32,256]{2,1,0:T(8,128)S(1)}, u32[]{:S(2)}, u32[]{:S(2)}) async-start(f32[16,32,256]{2,1,0:T(8,128)} %pad_maximum_fusion), calls=%async_computation.2 | async-start | bytes 1048576 | tf_op jit(solution)/shard_map/all_to_all | solution.py:192
  74.1 0.0 collective-permute-done.4
  74.1 2.2 %select_add_fusion = f32[768,256]{1,0:T(8,128)} fusion(f32[768,256]{1,0:T(8,128)} %collective-permute-done.4, f32[1536,256]{1,0:T(8,128)S(1)} %fusion.10, pred[]{:T(512)S(6)} %eq.34), kind=kLoop, calls=%fused_computation.8 | loop fusion | flops 393216 | bytes 3145729 | tf_op jit(solution)/shard_map/add | solution.py:247
  76.3 15.0 %all-to-all-done.2 = f32[16,32,256]{2,1,0:T(8,128)S(1)} async-done(((f32[16,32,256]{2,1,0:T(8,128)}), f32[16,32,256]{2,1,0:T(8,128)S(1)}, u32[]{:S(2)}, u32[]{:S(2)}) %all-to-all-start.2) | async-done | bytes 524320 | tf_op jit(solution)/shard_map/all_to_all | solution.py:192
  91.3 15.9 %all-gather = f32[512,256]{1,0:T(8,128)S(1)} all-gather(f32[32,256]{1,0:T(8,128)S(1)} %reduce_sum.18), channel_id=2, replica_groups=mesh['prow'=16,'pcol'=16] {'prow'}, dimensions={0}, use_global_device_ids=true | all-gather | bytes 557056 | tf_op jit(solution)/shard_map/all_gather | solution.py:248
  107.2 4.7 %all-to-all-start.3 = ((f32[8,96,256]{2,1,0:T(8,128)}), f32[8,96,256]{2,1,0:T(8,128)S(1)}, u32[]{:S(2)}, u32[]{:S(2)}) async-start(f32[8,96,256]{2,1,0:T(8,128)} %bitcast.12), calls=%async_computation.3 | async-start | bytes 1572864 | tf_op jit(solution)/shard_map/all_to_all | solution.py:192
  112.0 0.8 fusion.8
  112.8 14.2 %cholesky.1 = (f32[256,256]{1,0:T(8,128)}, f32[256,256]{1,0:T(8,128)}) custom-call(f32[256,256]{1,0:T(8,128)} %bitcast.42), custom_call_target="tpu_custom_call" | custom-call | flops 14000000000 | bytes 800000 | tf_op jit(solution)/shard_map/cholesky/pallas_call | solution.py:158
  127.0 8.6 %all-to-all-done.3 = f32[8,96,256]{2,1,0:T(8,128)S(1)} async-done(((f32[8,96,256]{2,1,0:T(8,128)}), f32[8,96,256]{2,1,0:T(8,128)S(1)}, u32[]{:S(2)}, u32[]{:S(2)}) %all-to-all-start.3) | async-done | bytes 786464 | tf_op jit(solution)/shard_map/all_to_all | solution.py:192
  135.6 0.1 reduce_sum.19
  135.7 1.2 convolution_add_fusion
  136.9 1.0 broadcast_in_dim.31
  137.8 3.5 %all-to-all-start.4 = ((f32[8,96,256]{2,1,0:T(8,128)}), f32[8,96,256]{2,1,0:T(8,128)S(1)}, u32[]{:S(2)}, u32[]{:S(2)}) async-start(f32[8,96,256]{2,1,0:T(8,128)} %broadcast_in_dim.31), calls=%async_computation.4 | async-start | bytes 1572864 | tf_op jit(solution)/shard_map/all_to_all | solution.py:192
  141.4 0.6 compare_reduce_fusion
  142.0 0.1 slice.109
  142.1 22.8 %all-to-all-done.4 = f32[8,96,256]{2,1,0:T(8,128)S(1)} async-done(((f32[8,96,256]{2,1,0:T(8,128)}), f32[8,96,256]{2,1,0:T(8,128)S(1)}, u32[]{:S(2)}, u32[]{:S(2)}) %all-to-all-start.4) | async-done | bytes 786464 | tf_op jit(solution)/shard_map/all_to_all | solution.py:192
  164.9 0.5 collective-permute-start.5
  165.4 17.0 %lower_upper.1 = (f32[256,256]{1,0:T(8,128)}, f32[2,128,128]{2,1,0:T(8,128)}, f32[256,256]{1,0:T(8,128)}) custom-call(f32[256,256]{1,0:T(8,128)} %bitcast.41, f32[256,256]{1,0:T(8,128)} %get-tuple-element.51.r_ref, f32[256,256]{1,0:T(8,128)} %get-tuple-element.52.inverse_ref), custom_call_target="tpu_custom_call" | custom-call | flops 16999999488 | bytes 1600000 | tf_op jit(solution)/shard_map/lower_upper/pallas_call | solution.py:170
  182.4 1.8 add_select_fusion
  184.2 1.6 fusion.11
  185.9 1.9 fusion.12
  187.8 0.2 maximum_select_fusion
  188.0 0.7 copy-done.3
  188.7 0.6 fusion.3
  189.4 4.6 %convolution_subtract_fusion = f32[1024,1536]{1,0:T(8,128)} fusion(f32[1024,1536]{1,0:T(8,128)S(1)} %copy-done, f32[256,1536]{1,0:T(8,128)S(1)} %fusion.3, f32[768,256]{1,0:T(8,128)S(1)} %slice.109, f32[256,256]{1,0:T(8,128)S(1)} %get-tuple-element.62), kind=kOutput, calls=%fused_computation | convolution fusion | flops 2417754112 | bytes 15204352 | tf_op jit(solution)/shard_map/dot_general | solution.py:182
  (21 shorter events, 0.2 us)
Async XLA Ops:
  2.9 1.4 slice-start
  5.7 8.9 %collective-permute-start = (f32[768,256]{1,0:T(8,128)}, f32[768,256]{1,0:T(8,128)}, u32[]{:S(2)}, u32[]{:S(2)}) collective-permute-start(f32[768,256]{1,0:T(8,128)} %split.17), channel_id=1, source_target_pairs={{0,16},{1,17},{2,18},{3,19},{4,20},{5,21},{6,22},{7,23},{8,24},{9,... | collective-permute-start | bytes 2359304 | tf_op jit(solution)/shard_map/ppermute | solution.py:209
  7.0 24.2 %all-to-all-start = ((f32[16,64,256]{2,1,0:T(8,128)}), f32[16,64,256]{2,1,0:T(8,128)S(1)}, u32[]{:S(2)}, u32[]{:S(2)}) async-start(f32[16,64,256]{2,1,0:T(8,128)} %bitcast), calls=%async_computation | async-start | bytes 2097152 | tf_op jit(solution)/shard_map/all_to_all | solution.py:192
  15.9 23.0 %collective-permute-start.1 = (f32[4,96,256]{2,1,0:T(8,128)S(1)}, f32[4,96,256]{2,1,0:T(8,128)S(1)}, u32[]{:S(2)}, u32[]{:S(2)}) collective-permute-start(f32[4,96,256]{2,1,0:T(8,128)S(1)} %bitcast.40), channel_id=1, source_target_pairs={{0,128},{16,144},{1,129},{17,145},{2,130},{18,146},{3,131},{19,147... | collective-permute-start | bytes 1179656 | tf_op jit(solution)/shard_map/ppermute | solution.py:209
  32.3 23.0 %all-to-all-start.1 = ((f32[16,64,256]{2,1,0:T(8,128)}), f32[16,64,256]{2,1,0:T(8,128)S(1)}, u32[]{:S(2)}, u32[]{:S(2)}) async-start(f32[16,64,256]{2,1,0:T(8,128)} %broadcast_in_dim.30), calls=%async_computation.1 | async-start | bytes 2097152 | tf_op jit(solution)/shard_map/all_to_all | solution.py:192
  39.1 4.7 %collective-permute-start.2 = (f32[2,96,256]{2,1,0:T(8,128)S(1)}, f32[2,96,256]{2,1,0:T(8,128)S(1)}, u32[]{:S(2)}, u32[]{:S(2)}) collective-permute-start(f32[2,96,256]{2,1,0:T(8,128)S(1)} %slice.115), channel_id=1, source_target_pairs={{0,64},{16,80},{128,192},{144,208},{1,65},{17,81},{129,193},{145,2... | collective-permute-start | bytes 589832 | tf_op jit(solution)/shard_map/ppermute | solution.py:209
  43.9 3.5 %collective-permute-start.3 = (f32[1,96,256]{2,1,0:T(8,128)S(1)}, f32[1,96,256]{2,1,0:T(8,128)S(1)}, u32[]{:S(2)}, u32[]{:S(2)}) collective-permute-start(f32[1,96,256]{2,1,0:T(8,128)S(1)} %slice.117), channel_id=1, source_target_pairs={{0,32},{16,48},{64,96},{80,112},{128,160},{144,176},{192,224},{208... | collective-permute-start | bytes 294920 | tf_op jit(solution)/shard_map/ppermute | solution.py:209
  66.2 7.8 %collective-permute-start.4 = (f32[768,256]{1,0:T(8,128)}, f32[768,256]{1,0:T(8,128)}, u32[]{:S(2)}, u32[]{:S(2)}) collective-permute-start(f32[768,256]{1,0:T(8,128)} %slice_select_fusion.1), channel_id=1, source_target_pairs={{0,16},{16,0},{32,48},{48,32},{64,80},{80,64},{96,112},{112,96},{1... | collective-permute-start | bytes 2359304 | tf_op jit(solution)/shard_map/ppermute | solution.py:209
  68.4 22.9 %all-to-all-start.2 = ((f32[16,32,256]{2,1,0:T(8,128)}), f32[16,32,256]{2,1,0:T(8,128)S(1)}, u32[]{:S(2)}, u32[]{:S(2)}) async-start(f32[16,32,256]{2,1,0:T(8,128)} %pad_maximum_fusion), calls=%async_computation.2 | async-start | bytes 1048576 | tf_op jit(solution)/shard_map/all_to_all | solution.py:192
  107.2 28.4 %all-to-all-start.3 = ((f32[8,96,256]{2,1,0:T(8,128)}), f32[8,96,256]{2,1,0:T(8,128)S(1)}, u32[]{:S(2)}, u32[]{:S(2)}) async-start(f32[8,96,256]{2,1,0:T(8,128)} %bitcast.12), calls=%async_computation.3 | async-start | bytes 1572864 | tf_op jit(solution)/shard_map/all_to_all | solution.py:192
  137.8 27.0 %all-to-all-start.4 = ((f32[8,96,256]{2,1,0:T(8,128)}), f32[8,96,256]{2,1,0:T(8,128)S(1)}, u32[]{:S(2)}, u32[]{:S(2)}) async-start(f32[8,96,256]{2,1,0:T(8,128)} %broadcast_in_dim.31), calls=%async_computation.4 | async-start | bytes 1572864 | tf_op jit(solution)/shard_map/all_to_all | solution.py:192
  164.9 21.0 %collective-permute-start.5 = (f32[768,256]{1,0:T(8,128)S(1)}, f32[768,256]{1,0:T(8,128)}, u32[]{:S(2)}, u32[]{:S(2)}) collective-permute-start(f32[768,256]{1,0:T(8,128)S(1)} %bitcast.34), channel_id=1, source_target_pairs={{0,16},{16,0},{32,48},{48,32},{64,80},{80,64},{96,112},{112,96},{1... | collective-permute-start | bytes 2359304 | tf_op jit(solution)/shard_map/ppermute | solution.py:209
  165.4 17.0 %copy-start.2 = (f32[256,256]{1,0:T(8,128)S(1)}, f32[256,256]{1,0:T(8,128)}, u32[]{:S(2)}) copy-start(f32[256,256]{1,0:T(8,128)} %get-tuple-element.51.r_ref) | copy-start | bytes 786436
  182.4 3.4 %copy-start.1 = (f32[256,256]{1,0:T(8,128)S(1)}, f32[256,256]{1,0:T(8,128)}, u32[]{:S(2)}) copy-start(f32[256,256]{1,0:T(8,128)} %get-tuple-element.53) | copy-start | bytes 786436
  184.2 5.1 %copy-start = (f32[1024,1536]{1,0:T(8,128)S(1)}, f32[1024,1536]{1,0:T(8,128)}, u32[]{:S(2)}) copy-start(f32[1024,1536]{1,0:T(8,128)} %get-tuple-element.63) | copy-start | bytes 18874372
  187.8 1.0 copy-start.3
where the time goes:
time: 195 us; the launch traced here: 194 us
  waiting for transfers between devices  59.1 us (30%)
  starting transfers between devices  44.7 us (23%)
  Pallas kernels  31.2 us (16%)
  matrix products  18.4 us (9%)
  blocking collectives  15.9 us (8%)
  other arithmetic  14.9 us (8%)
  local copies, waits for them, and re-layouts  8.84 us (5%)
    all_to_all x5, waiting for transfers between devices, exchange(): return lax.all_to_all(pieces, axis, 0, 0, axis_index_groups=groups)  54.3 us
    all_to_all x5, starting transfers between devices, exchange(): return lax.all_to_all(pieces, axis, 0, 0, axis_index_groups=groups)  28.2 us
    pallas_call x1, Pallas kernels, lower_upper(): pl.pallas_call(lower_upper_kernel, out_shape=(square_shape, jax.ShapeDtyp...  17 us
    ppermute x6, starting transfers between devices, permute(): return lax.ppermute(value, 'prow', pairs)  16.5 us
    all_gather x1, blocking collectives, per_device(): lax.all_gather(square_piece, 'prow')  15.9 us
    pallas_call x1, Pallas kernels, cholesky(): pl.pallas_call(cholesky_kernel, out_shape=(square_shape,) * 2, scratch_sh...  14.2 us
    dot_general x2, matrix products, transposed_product(): lax.dot_general(left, right, (((0,), (0,)), ((), ())), precision=precisio...  9.02 us
    select_n x1, other arithmetic, per_device(): base = jnp.where(replaced, 0.0, source)  6.16 us
  transfers between devices with their start and end apart: 11, of which 6 were waited for; matrix products, arithmetic and copies ran while one was open for 8% of the time, Pallas kernels for 16%

commit v1 on v0

--- a/solution.py
+++ b/solution.py
@@ -3,6 +3,7 @@
 from jax import lax
 from jax.experimental import pallas as pl
 from jax.experimental.pallas import tpu as pltpu
+from jax.experimental.layout import Layout, with_layout_constraint
 from jax.sharding import PartitionSpec as P
 
 
@@ -217,13 +218,9 @@
 
     column_ids = lax.broadcasted_iota(jnp.int32, (1, cols), 1)
     replaced = has_panel & (column_ids < WIDE)
-    pieces, top_rows, source = lax.optimization_barrier(
-        (matrix[:, :WIDE].reshape(cols_count, -1, WIDE), matrix[:WIDE], matrix)
-    )
+    pieces = matrix[:, :WIDE].reshape(cols_count, -1, WIDE)
     panel_piece = exchange(pieces, "pcol")[0]
-    base = jnp.where(replaced, 0.0, source)
-    low, high_half = jnp.split(top_rows.T, CORES)
-    panel_piece, base = lax.optimization_barrier((panel_piece, base))
+    low, high_half = jnp.split(matrix[:WIDE].T, CORES)
     panel = gather(panel_piece, "pcol", cols_count).reshape(rows, WIDE)
 
     top_half = jnp.where(core == 0, low, permute(high_half, [(0, 1)]))
@@ -237,17 +234,21 @@
         step //= 2
     panel, top_slice = lax.optimization_barrier((panel, held[0]))
 
-    own_top = jnp.where(on_top, panel[:WIDE], 0.0)
-    squares = [transposed_product(panel, panel), own_top]
-    squares = jnp.concatenate([a.reshape(rows_count, -1, WIDE) for a in squares], axis=1)
-    squares, panel = lax.optimization_barrier((squares, panel))
-    square_piece = exchange(squares, "prow")
-    mine, other = halves(transposed_product(base, panel, high))
-    square_piece = square_piece.sum(0)
-    mine = mine + swap(other)
-    squares, mine = lax.optimization_barrier((lax.all_gather(square_piece, "prow"), mine))
+    strip = WIDE // cols_count
+    squares = [
+        lax.dynamic_slice_in_dim(a, my_col * strip, strip, 0)
+        for a in (transposed_product(panel, panel), panel)
+    ]
+    squares = jnp.concatenate([squares[0], jnp.where(on_top, squares[1], 0.0)], axis=0)
+    square_piece, panel = lax.optimization_barrier((lax.all_gather(squares, "prow"), panel))
+    squares = gather(square_piece.sum(0), "pcol", cols_count)
+    mine, other = halves(transposed_product(matrix, panel, high))
+    mine = with_layout_constraint(mine + swap(other), Layout((0, 1)))
+    squares, mine = lax.optimization_barrier((squares, mine))
     gram, top = (a.reshape(WIDE, WIDE) for a in jnp.split(squares, 2, axis=1))
-    summed = exchange(mine.reshape(LEVELS, -1, WIDE), "prow", levels).sum(0)
+    summed = exchange(mine.reshape(LEVELS, -1, WIDE), "prow", levels)
+    base = lax.optimization_barrier(jnp.where(replaced, 0.0, matrix))
+    summed = summed.sum(0)
     upper, inverse = cholesky(gram)
     summed = summed + product(top_slice, upper)
     summed = gather(summed, "prow", LEVELS, levels).reshape(-1, WIDE)

time: 195 us -> 191 us (0.979)
  waiting for transfers between devices: 59.1 us -> 49.4 us
  blocking collectives: 15.9 us -> 24.5 us
  starting transfers between devices: 44.7 us -> 40.2 us
  local copies, waits for them, and re-layouts: 8.84 us -> 12.3 us
    all_to_all x5, waiting for transfers between devices: 54.3 us -> 44.6 us  [exchange(): return lax.all_to_all(pieces, axis, 0, 0, axis_index_groups=groups)]
    all_gather x1, blocking collectives: 15.9 us -> 24.5 us  [per_device(): lax.all_gather(squares, 'prow')]
    all_to_all x5, starting transfers between devices: 28.2 us -> 24 us  [exchange(): return lax.all_to_all(pieces, axis, 0, 0, axis_index_groups=groups)]
    slice x3 -> x2, local copies, waits for them, and re-layouts: 3.68 us -> 4.92 us  [the longest x1 2.66 us: per_device(): low, high_half = jnp.split(matrix[:WIDE].T, CORES)]
  transfers between devices with their start and end apart: 11 -> 11, of which waited for: 6 -> 7; matrix products, arithmetic and copies ran while one was open for 8% -> 10% of each run, Pallas kernels for 16% -> 16%
where the time goes in v1:
time: 191 us; the launch traced here: 190 us
  waiting for transfers between devices  49.4 us (26%)
  starting transfers between devices  40.2 us (21%)
  Pallas kernels  31.2 us (16%)
  blocking collectives  24.5 us (13%)
  matrix products  18.4 us (10%)
  other arithmetic  13.1 us (7%)
  local copies, waits for them, and re-layouts  12.3 us (6%)
    all_to_all x5, waiting for transfers between devices, exchange(): return lax.all_to_all(pieces, axis, 0, 0, axis_index_groups=groups)  44.6 us
    all_gather x1, blocking collectives, per_device(): lax.all_gather(squares, 'prow')  24.5 us
    all_to_all x5, starting transfers between devices, exchange(): return lax.all_to_all(pieces, axis, 0, 0, axis_index_groups=groups)  24 us
    pallas_call x1, Pallas kernels, lower_upper(): pl.pallas_call(lower_upper_kernel, out_shape=(square_shape, jax.ShapeDtyp...  17 us
    ppermute x6, starting transfers between devices, permute(): return lax.ppermute(value, 'prow', pairs)  16.2 us
    pallas_call x1, Pallas kernels, cholesky(): pl.pallas_call(cholesky_kernel, out_shape=(square_shape,) * 2, scratch_sh...  14.2 us
    dot_general x2, matrix products, transposed_product(): lax.dot_general(left, right, (((0,), (0,)), ((), ())), precision=precisio...  9.04 us
    select_n x1, other arithmetic, per_device(): base = lax.optimization_barrier(jnp.where(replaced, 0.0, matrix))  6.16 us
  transfers between devices with their start and end apart: 11, of which 7 were waited for; matrix products, arithmetic and copies ran while one was open for 10% of the time, Pallas kernels for 16%

profile of v1, /device:TPU:1, one launch (start us, length us, event | category | flops | bytes accessed | tf_op | source)
XLA Modules:
  0.0 190.1 jit_solution(2844352431662580579)
XLA Ops:
  0.6 2.7 %slice.92 = f32[256,1536]{1,0:T(8,128)} slice(f32[1024,1536]{1,0:T(8,128)} %param.5), slice={[0:256], [0:1536]} | slice | bytes 3145728 | tf_op jit(solution)/shard_map/slice | solution.py:223
  3.3 1.9 copy.6
  5.2 0.1 split.17
  5.2 1.3 collective-permute-start
  6.5 2.3 %slice.90 = f32[1024,256]{1,0:T(8,128)} slice(f32[1024,1536]{1,0:T(8,128)} %param.5), slice={[0:1024], [0:256]} | slice | bytes 2097152 | tf_op jit(solution)/shard_map/slice | solution.py:221
  8.8 7.6 %all-to-all-start = ((f32[16,64,256]{2,1,0:T(8,128)}), f32[16,64,256]{2,1,0:T(8,128)}, u32[]{:S(2)}, u32[]{:S(2)}) async-start(f32[16,64,256]{2,1,0:T(8,128)} %bitcast), calls=%async_computation | async-start | bytes 2097152 | tf_op jit(solution)/shard_map/all_to_all | solution.py:193
  16.4 0.1 slice_select_fusion
  16.6 0.1 fusion.8
  16.6 8.3 %collective-permute-start.1 = (f32[4,96,256]{2,1,0:T(8,128)S(1)}, f32[4,96,256]{2,1,0:T(8,128)S(1)}, u32[]{:S(2)}, u32[]{:S(2)}) collective-permute-start(f32[4,96,256]{2,1,0:T(8,128)S(1)} %bitcast.38), channel_id=1, source_target_pairs={{0,128},{16,144},{1,129},{17,145},{2,130},{18,146},{3,131},{19,147... | collective-permute-start | bytes 1179656 | tf_op jit(solution)/shard_map/ppermute | solution.py:210
  24.9 7.1 %all-to-all-done = f32[16,64,256]{2,1,0:T(8,128)} async-done(((f32[16,64,256]{2,1,0:T(8,128)}), f32[16,64,256]{2,1,0:T(8,128)}, u32[]{:S(2)}, u32[]{:S(2)}) %all-to-all-start) | async-done | bytes 1048608 | tf_op jit(solution)/shard_map/all_to_all | solution.py:193
  32.0 0.8 slice_bitcast_fusion
  32.9 1.1 broadcast_in_dim.35
  33.9 4.3 %all-to-all-start.1 = ((f32[16,64,256]{2,1,0:T(8,128)}), f32[16,64,256]{2,1,0:T(8,128)S(1)}, u32[]{:S(2)}, u32[]{:S(2)}) async-start(f32[16,64,256]{2,1,0:T(8,128)} %broadcast_in_dim.35), calls=%async_computation.1 | async-start | bytes 2097152 | tf_op jit(solution)/shard_map/all_to_all | solution.py:193
  38.3 0.1 broadcast_select_fusion.1
  38.4 4.7 %collective-permute-start.2 = (f32[2,96,256]{2,1,0:T(8,128)S(1)}, f32[2,96,256]{2,1,0:T(8,128)S(1)}, u32[]{:S(2)}, u32[]{:S(2)}) collective-permute-start(f32[2,96,256]{2,1,0:T(8,128)S(1)} %slice.111), channel_id=1, source_target_pairs={{0,64},{16,80},{128,192},{144,208},{1,65},{17,81},{129,193},{145,2... | collective-permute-start | bytes 589832 | tf_op jit(solution)/shard_map/ppermute | solution.py:210
  43.1 2.6 %collective-permute-done.2 = f32[2,96,256]{2,1,0:T(8,128)S(1)} collective-permute-done((f32[2,96,256]{2,1,0:T(8,128)S(1)}, f32[2,96,256]{2,1,0:T(8,128)S(1)}, u32[]{:S(2)}, u32[]{:S(2)}) %collective-permute-start.2) | collective-permute-done | bytes 196640 | tf_op jit(solution)/shard_map/ppermute | solution.py:210
  45.7 1.3 collective-permute-start.3
  47.0 2.2 %collective-permute-done.3 = f32[1,96,256]{2,1,0:T(8,128)S(1)} collective-permute-done((f32[1,96,256]{2,1,0:T(8,128)S(1)}, f32[1,96,256]{2,1,0:T(8,128)S(1)}, u32[]{:S(2)}, u32[]{:S(2)}) %collective-permute-start.3) | collective-permute-done | bytes 98336 | tf_op jit(solution)/shard_map/ppermute | solution.py:210
  49.2 4.0 %all-to-all-done.1 = f32[16,64,256]{2,1,0:T(8,128)S(1)} async-done(((f32[16,64,256]{2,1,0:T(8,128)}), f32[16,64,256]{2,1,0:T(8,128)S(1)}, u32[]{:S(2)}, u32[]{:S(2)}) %all-to-all-start.1) | async-done | bytes 1048608 | tf_op jit(solution)/shard_map/all_to_all | solution.py:193
  53.2 1.8 fusion.10
  55.1 24.5 %all-gather = f32[512,256]{1,0:T(8,128)S(1)} all-gather(f32[32,256]{1,0:T(8,128)S(1)} %pad_maximum_fusion), channel_id=2, replica_groups=mesh['prow'=16,'pcol'=16] {'prow'}, dimensions={0}, use_global_device_ids=true | all-gather | bytes 557056 | tf_op jit(solution)/shard_map/all_gather | solution.py:243
  79.5 7.2 %convolution_bitcast_fusion = f32[1536,256]{1,0:T(8,128)S(1)} fusion(f32[1024,256]{1,0:T(8,128)S(1)} %bitcast.29, f32[1024,1536]{1,0:T(8,128)} %param.5), kind=kOutput, calls=%fused_computation.2 | convolution fusion | flops 2415919104 | bytes 8912896 | tf_op jit(solution)/shard_map/dot_general | solution.py:187
  86.8 1.0 slice_select_fusion.1
  87.7 0.2 collective-permute-start.4
  87.9 0.9 broadcast_in_dim.37
  88.8 5.0 %all-to-all-start.2 = ((f32[16,32,256]{2,1,0:T(8,128)}), f32[16,32,256]{2,1,0:T(8,128)S(1)}, u32[]{:S(2)}, u32[]{:S(2)}) async-start(f32[16,32,256]{2,1,0:T(8,128)} %broadcast_in_dim.37), calls=%async_computation.2 | async-start | bytes 1048576 | tf_op jit(solution)/shard_map/all_to_all | solution.py:193
  93.8 2.2 %select_add_fusion = f32[768,256]{1,0:T(8,128)} fusion(f32[768,256]{1,0:T(8,128)} %collective-permute-done.4, f32[1536,256]{1,0:T(8,128)S(1)} %convolution_bitcast_fusion, pred[]{:T(512)S(6)} %eq.34), kind=kLoop, calls=%fused_computation.9 | loop fusion | flops 393216 | bytes 3145729 | tf_op jit(solution)/shard_map/add | solution.py:246
  95.9 8.6 %all-to-all-done.2 = f32[16,32,256]{2,1,0:T(8,128)S(1)} async-done(((f32[16,32,256]{2,1,0:T(8,128)}), f32[16,32,256]{2,1,0:T(8,128)S(1)}, u32[]{:S(2)}, u32[]{:S(2)}) %all-to-all-start.2) | async-done | bytes 524320 | tf_op jit(solution)/shard_map/all_to_all | solution.py:193
  104.5 3.5 %all-to-all-start.3 = ((f32[8,96,256]{2,1,0:T(8,128)}), f32[8,96,256]{2,1,0:T(8,128)S(1)}, u32[]{:S(2)}, u32[]{:S(2)}) async-start(f32[8,96,256]{2,1,0:T(8,128)} %bitcast.11), calls=%async_computation.3 | async-start | bytes 1572864 | tf_op jit(solution)/shard_map/all_to_all | solution.py:193
  108.1 0.8 fusion.9
  108.9 14.2 %cholesky.1 = (f32[256,256]{1,0:T(8,128)}, f32[256,256]{1,0:T(8,128)}) custom-call(f32[256,256]{1,0:T(8,128)} %bitcast.40), custom_call_target="tpu_custom_call" | custom-call | flops 14000000000 | bytes 800000 | tf_op jit(solution)/shard_map/cholesky/pallas_call | solution.py:159
  123.1 8.4 %all-to-all-done.3 = f32[8,96,256]{2,1,0:T(8,128)S(1)} async-done(((f32[8,96,256]{2,1,0:T(8,128)}), f32[8,96,256]{2,1,0:T(8,128)S(1)}, u32[]{:S(2)}, u32[]{:S(2)}) %all-to-all-start.3) | async-done | bytes 786464 | tf_op jit(solution)/shard_map/all_to_all | solution.py:193
  131.6 1.2 convolution_add_fusion
  132.8 1.0 broadcast_in_dim.38
  133.8 3.5 %all-to-all-start.4 = ((f32[8,96,256]{2,1,0:T(8,128)}), f32[8,96,256]{2,1,0:T(8,128)S(1)}, u32[]{:S(2)}, u32[]{:S(2)}) async-start(f32[8,96,256]{2,1,0:T(8,128)} %broadcast_in_dim.38), calls=%async_computation.4 | async-start | bytes 1572864 | tf_op jit(solution)/shard_map/all_to_all | solution.py:193
  137.4 6.2 %broadcast_select_fusion = f32[1024,1536]{1,0:T(8,128)} fusion(f32[1024,1536]{1,0:T(8,128)} %param.5, pred[1536]{0:T(1024)(128)(4,1)S(1)} %fusion.6), kind=kLoop, calls=%fused_computation.1 | loop fusion | flops 1572864 | bytes 12584448 | tf_op jit(solution)/shard_map/jit(_where)/select_n | solution.py:250
  143.5 0.7 compare_reduce_fusion
  144.2 0.1 slice.105
  144.3 16.5 %all-to-all-done.4 = f32[8,96,256]{2,1,0:T(8,128)S(1)} async-done(((f32[8,96,256]{2,1,0:T(8,128)}), f32[8,96,256]{2,1,0:T(8,128)S(1)}, u32[]{:S(2)}, u32[]{:S(2)}) %all-to-all-start.4) | async-done | bytes 786464 | tf_op jit(solution)/shard_map/all_to_all | solution.py:193
  160.8 0.5 collective-permute-start.5
  161.3 17.0 %lower_upper.1 = (f32[256,256]{1,0:T(8,128)}, f32[2,128,128]{2,1,0:T(8,128)}, f32[256,256]{1,0:T(8,128)}) custom-call(f32[256,256]{1,0:T(8,128)} %bitcast.39, f32[256,256]{1,0:T(8,128)} %get-tuple-element.41.r_ref, f32[256,256]{1,0:T(8,128)} %get-tuple-element.42.inverse_ref), custom_call_target="tpu_custom_call" | custom-call | flops 16999999488 | bytes 1600000 | tf_op jit(solution)/shard_map/lower_upper/pallas_call | solution.py:171
  178.4 1.8 add_select_fusion
  180.2 1.6 fusion.11
  181.8 1.9 fusion.12
  183.7 0.2 maximum_select_fusion
  183.9 0.7 copy-done.3
  184.7 0.8 fusion.3
  185.5 4.6 %convolution_subtract_fusion = f32[1024,1536]{1,0:T(8,128)} fusion(f32[1024,1536]{1,0:T(8,128)S(1)} %copy-done, f32[256,1536]{1,0:T(8,128)S(1)} %fusion.3, f32[768,256]{1,0:T(8,128)S(1)} %slice.105, f32[256,256]{1,0:T(8,128)S(1)} %get-tuple-element.52), kind=kOutput, calls=%fused_computation | convolution fusion | flops 2417754112 | bytes 15204352 | tf_op jit(solution)/shard_map/dot_general | solution.py:183
  (21 shorter events, 0.2 us)
Async XLA Ops:
  5.2 11.2 %collective-permute-start = (f32[768,256]{1,0:T(8,128)S(1)}, f32[768,256]{1,0:T(8,128)S(1)}, u32[]{:S(2)}, u32[]{:S(2)}) collective-permute-start(f32[768,256]{1,0:T(8,128)S(1)} %split.17), channel_id=1, source_target_pairs={{0,16},{1,17},{2,18},{3,19},{4,20},{5,21},{6,22},{7,23},{8,24},{9,... | collective-permute-start | bytes 2359304 | tf_op jit(solution)/shard_map/ppermute | solution.py:210
  8.8 23.2 %all-to-all-start = ((f32[16,64,256]{2,1,0:T(8,128)}), f32[16,64,256]{2,1,0:T(8,128)}, u32[]{:S(2)}, u32[]{:S(2)}) async-start(f32[16,64,256]{2,1,0:T(8,128)} %bitcast), calls=%async_computation | async-start | bytes 2097152 | tf_op jit(solution)/shard_map/all_to_all | solution.py:193
  16.6 21.6 %collective-permute-start.1 = (f32[4,96,256]{2,1,0:T(8,128)S(1)}, f32[4,96,256]{2,1,0:T(8,128)S(1)}, u32[]{:S(2)}, u32[]{:S(2)}) collective-permute-start(f32[4,96,256]{2,1,0:T(8,128)S(1)} %bitcast.38), channel_id=1, source_target_pairs={{0,128},{16,144},{1,129},{17,145},{2,130},{18,146},{3,131},{19,147... | collective-permute-start | bytes 1179656 | tf_op jit(solution)/shard_map/ppermute | solution.py:210
  33.9 19.2 %all-to-all-start.1 = ((f32[16,64,256]{2,1,0:T(8,128)}), f32[16,64,256]{2,1,0:T(8,128)S(1)}, u32[]{:S(2)}, u32[]{:S(2)}) async-start(f32[16,64,256]{2,1,0:T(8,128)} %broadcast_in_dim.35), calls=%async_computation.1 | async-start | bytes 2097152 | tf_op jit(solution)/shard_map/all_to_all | solution.py:193
  38.4 7.3 %collective-permute-start.2 = (f32[2,96,256]{2,1,0:T(8,128)S(1)}, f32[2,96,256]{2,1,0:T(8,128)S(1)}, u32[]{:S(2)}, u32[]{:S(2)}) collective-permute-start(f32[2,96,256]{2,1,0:T(8,128)S(1)} %slice.111), channel_id=1, source_target_pairs={{0,64},{16,80},{128,192},{144,208},{1,65},{17,81},{129,193},{145,2... | collective-permute-start | bytes 589832 | tf_op jit(solution)/shard_map/ppermute | solution.py:210
  45.7 3.5 %collective-permute-start.3 = (f32[1,96,256]{2,1,0:T(8,128)S(1)}, f32[1,96,256]{2,1,0:T(8,128)S(1)}, u32[]{:S(2)}, u32[]{:S(2)}) collective-permute-start(f32[1,96,256]{2,1,0:T(8,128)S(1)} %slice.113), channel_id=1, source_target_pairs={{0,32},{16,48},{64,96},{80,112},{128,160},{144,176},{192,224},{208... | collective-permute-start | bytes 294920 | tf_op jit(solution)/shard_map/ppermute | solution.py:210
  87.7 6.0 %collective-permute-start.4 = (f32[768,256]{1,0:T(8,128)}, f32[768,256]{1,0:T(8,128)}, u32[]{:S(2)}, u32[]{:S(2)}) collective-permute-start(f32[768,256]{1,0:T(8,128)} %slice_select_fusion.1), channel_id=1, source_target_pairs={{0,16},{16,0},{32,48},{48,32},{64,80},{80,64},{96,112},{112,96},{1... | collective-permute-start | bytes 2359304 | tf_op jit(solution)/shard_map/ppermute | solution.py:210
  88.8 15.7 %all-to-all-start.2 = ((f32[16,32,256]{2,1,0:T(8,128)}), f32[16,32,256]{2,1,0:T(8,128)S(1)}, u32[]{:S(2)}, u32[]{:S(2)}) async-start(f32[16,32,256]{2,1,0:T(8,128)} %broadcast_in_dim.37), calls=%async_computation.2 | async-start | bytes 1048576 | tf_op jit(solution)/shard_map/all_to_all | solution.py:193
  104.5 27.0 %all-to-all-start.3 = ((f32[8,96,256]{2,1,0:T(8,128)}), f32[8,96,256]{2,1,0:T(8,128)S(1)}, u32[]{:S(2)}, u32[]{:S(2)}) async-start(f32[8,96,256]{2,1,0:T(8,128)} %bitcast.11), calls=%async_computation.3 | async-start | bytes 1572864 | tf_op jit(solution)/shard_map/all_to_all | solution.py:193
  133.8 27.0 %all-to-all-start.4 = ((f32[8,96,256]{2,1,0:T(8,128)}), f32[8,96,256]{2,1,0:T(8,128)S(1)}, u32[]{:S(2)}, u32[]{:S(2)}) async-start(f32[8,96,256]{2,1,0:T(8,128)} %broadcast_in_dim.38), calls=%async_computation.4 | async-start | bytes 1572864 | tf_op jit(solution)/shard_map/all_to_all | solution.py:193
  160.8 21.0 %collective-permute-start.5 = (f32[768,256]{1,0:T(8,128)S(1)}, f32[768,256]{1,0:T(8,128)}, u32[]{:S(2)}, u32[]{:S(2)}) collective-permute-start(f32[768,256]{1,0:T(8,128)S(1)} %bitcast.34), channel_id=1, source_target_pairs={{0,16},{16,0},{32,48},{48,32},{64,80},{80,64},{96,112},{112,96},{1... | collective-permute-start | bytes 2359304 | tf_op jit(solution)/shard_map/ppermute | solution.py:210
  161.3 17.1 %copy-start.2 = (f32[256,256]{1,0:T(8,128)S(1)}, f32[256,256]{1,0:T(8,128)}, u32[]{:S(2)}) copy-start(f32[256,256]{1,0:T(8,128)} %get-tuple-element.41.r_ref) | copy-start | bytes 786436
  178.4 3.4 %copy-start.1 = (f32[256,256]{1,0:T(8,128)S(1)}, f32[256,256]{1,0:T(8,128)}, u32[]{:S(2)}) copy-start(f32[256,256]{1,0:T(8,128)} %get-tuple-element.43) | copy-start | bytes 786436
  180.2 5.3 %copy-start = (f32[1024,1536]{1,0:T(8,128)S(1)}, f32[1024,1536]{1,0:T(8,128)}, u32[]{:S(2)}) copy-start(f32[1024,1536]{1,0:T(8,128)} %get-tuple-element.53) | copy-start | bytes 18874372
  183.7 1.0 copy-start.3

commit v2 on v1

--- a/solution.py
+++ b/solution.py
@@ -3,7 +3,6 @@
 from jax import lax
 from jax.experimental import pallas as pl
 from jax.experimental.pallas import tpu as pltpu
-from jax.experimental.layout import Layout, with_layout_constraint
 from jax.sharding import PartitionSpec as P
 
 
@@ -189,6 +188,26 @@
     )
 
 
+def join_kernel(flags, products_ref, received_ref, joined_ref):
+    width = received_ref.shape[1]
+    half = jnp.where(flags[0] == 0, products_ref[:, :width], products_ref[:, width:])
+    joined_ref[...] = (half + received_ref[...]).T
+
+
+def joined(core, products, received):
+    vmem = pl.BlockSpec(memory_space=pltpu.VMEM)
+    return pl.pallas_call(
+        join_kernel,
+        in_specs=[pl.BlockSpec(memory_space=pltpu.SMEM), vmem, vmem],
+        out_specs=vmem,
+        out_shape=jax.ShapeDtypeStruct(received.shape[::-1], f32),
+        cost_estimate=pl.CostEstimate(
+            flops=1_000_000_000, bytes_accessed=4_000_000, transcendentals=0
+        ),
+        name="join",
+    )(core.reshape(1), products, received)
+
+
 def exchange(pieces, axis, groups=None):
     return lax.all_to_all(pieces, axis, 0, 0, axis_index_groups=groups)
 
@@ -211,10 +230,6 @@
 
     def swap(value):
         return permute(value, [(i, i ^ 1) for i in range(rows_count)])
-
-    def halves(value):
-        low, high = value[: value.shape[0] // CORES], value[value.shape[0] // CORES :]
-        return jnp.where(core == 0, low, high), jnp.where(core == 0, high, low)
 
     column_ids = lax.broadcasted_iota(jnp.int32, (1, cols), 1)
     replaced = has_panel & (column_ids < WIDE)
@@ -240,14 +255,17 @@
         for a in (transposed_product(panel, panel), panel)
     ]
     squares = jnp.concatenate([squares[0], jnp.where(on_top, squares[1], 0.0)], axis=0)
-    square_piece, panel = lax.optimization_barrier((lax.all_gather(squares, "prow"), panel))
-    squares = gather(square_piece.sum(0), "pcol", cols_count)
-    mine, other = halves(transposed_product(matrix, panel, high))
-    mine = with_layout_constraint(mine + swap(other), Layout((0, 1)))
+    squares, panel = lax.optimization_barrier((squares + swap(squares), panel))
+    squares = gather(squares, "prow", LEVELS, levels)
+    products = transposed_product(panel, matrix, high)
+    low_half, high_half = jnp.split(products, CORES, axis=1)
+    other = jnp.where(core == 0, high_half, low_half)
+    squares = gather(squares.sum(0), "pcol", cols_count)
+    base = lax.optimization_barrier(jnp.where(replaced, 0.0, matrix))
+    mine = joined(core, products, swap(other))
     squares, mine = lax.optimization_barrier((squares, mine))
+    summed = exchange(mine.reshape(LEVELS, -1, WIDE), "prow", levels)
     gram, top = (a.reshape(WIDE, WIDE) for a in jnp.split(squares, 2, axis=1))
-    summed = exchange(mine.reshape(LEVELS, -1, WIDE), "prow", levels)
-    base = lax.optimization_barrier(jnp.where(replaced, 0.0, matrix))
     summed = summed.sum(0)
     upper, inverse = cholesky(gram)
     summed = summed + product(top_slice, upper)

time: 191 us -> 178 us (0.932)
  blocking collectives: 24.5 us -> 0 us
  starting transfers between devices: 40.2 us -> 53.5 us
  Pallas kernels: 31.2 us -> 34 us
  other arithmetic: 13.1 us -> 10.9 us
  matrix products: 18.4 us -> 16.3 us
    all_gather x1 -> x0, blocking collectives: 24.5 us -> none  [per_device(): lax.all_gather(squares, 'prow')]
    ppermute x6 -> x7, starting transfers between devices: 16.2 us -> 23 us  [permute(): return lax.ppermute(value, 'prow', pairs)]
    all_to_all x5 -> x6, starting transfers between devices: 24 us -> 30.5 us  [exchange(): return lax.all_to_all(pieces, axis, 0, 0, axis_index_groups=groups)]
    pallas_call x0 -> x1, Pallas kernels: none -> 2.76 us  [joined(): pl.pallas_call(join_kernel, in_specs=[pl.BlockSpec(memory_space=pltpu.SME...]
    add x1, other arithmetic: 2.16 us -> 0.01 us  [per_device(): squares, panel = lax.optimization_barrier((squares + swap(squares), panel))]
    dot_general x2, matrix products: 9.04 us -> 6.94 us  [transposed_product(): lax.dot_general(left, right, (((0,), (0,)), ((), ())), precision=precisio...]
    all_to_all x5 -> x6, waiting for transfers between devices: 44.6 us -> 42.6 us  [exchange(): return lax.all_to_all(pieces, axis, 0, 0, axis_index_groups=groups)]
    ppermute x6 -> x7, waiting for transfers between devices: 4.76 us -> 5.62 us  [permute(): return lax.ppermute(value, 'prow', pairs)]
  transfers between devices with their start and end apart: 11 -> 13, of which waited for: 7 -> 9; matrix products, arithmetic and copies ran while one was open for 10% -> 13% of each run, Pallas kernels for 16% -> 19%
where the time goes in v2:
time: 178 us; the launch traced here: 177 us
  starting transfers between devices  53.5 us (30%)
  waiting for transfers between devices  48.2 us (27%)
  Pallas kernels  34 us (19%)
  matrix products  16.3 us (9%)
  local copies, waits for them, and re-layouts  13 us (7%)
  other arithmetic  10.9 us (6%)
    all_to_all x6, waiting for transfers between devices, exchange(): return lax.all_to_all(pieces, axis, 0, 0, axis_index_groups=groups)  42.6 us
    all_to_all x6, starting transfers between devices, exchange(): return lax.all_to_all(pieces, axis, 0, 0, axis_index_groups=groups)  30.5 us
    ppermute x7, starting transfers between devices, permute(): return lax.ppermute(value, 'prow', pairs)  23 us
    pallas_call x1, Pallas kernels, lower_upper(): pl.pallas_call(lower_upper_kernel, out_shape=(square_shape, jax.ShapeDtyp...  17 us
    pallas_call x1, Pallas kernels, cholesky(): pl.pallas_call(cholesky_kernel, out_shape=(square_shape,) * 2, scratch_sh...  14.2 us
    dot_general x2, matrix products, transposed_product(): lax.dot_general(left, right, (((0,), (0,)), ((), ())), precision=precisio...  6.94 us
    select_n x1, other arithmetic, per_device(): base = lax.optimization_barrier(jnp.where(replaced, 0.0, matrix))  6.16 us
    dot_general x2, matrix products, product(): return jnp.dot(left, right, precision=precision, preferred_element_type=f32)  5.84 us
  transfers between devices with their start and end apart: 13, of which 9 were waited for; matrix products, arithmetic and copies ran while one was open for 13% of the time, Pallas kernels for 19%

profile of v2, /device:TPU:1, one launch (start us, length us, event | category | flops | bytes accessed | tf_op | source)
XLA Modules:
  0.0 177.0 jit_solution(14904181740991816300)
XLA Ops:
  0.6 2.7 %slice.86 = f32[256,1536]{1,0:T(8,128)} slice(f32[1024,1536]{1,0:T(8,128)} %param.5), slice={[0:256], [0:1536]} | slice | bytes 3145728 | tf_op jit(solution)/shard_map/slice | solution.py:238
  3.3 1.9 %copy.5 = f32[256,1536]{0,1:T(8,128)S(1)} copy(f32[256,1536]{1,0:T(8,128)} %slice.86) | data formatting | bytes 3145728
  5.2 1.3 collective-permute-start
  6.5 2.3 %slice.84 = f32[1024,256]{1,0:T(8,128)} slice(f32[1024,1536]{1,0:T(8,128)} %param.5), slice={[0:1024], [0:256]} | slice | bytes 2097152 | tf_op jit(solution)/shard_map/slice | solution.py:236
  8.8 7.6 %all-to-all-start = ((f32[16,64,256]{2,1,0:T(8,128)}), f32[16,64,256]{2,1,0:T(8,128)}, u32[]{:S(2)}, u32[]{:S(2)}) async-start(f32[16,64,256]{2,1,0:T(8,128)} %bitcast), calls=%async_computation | async-start | bytes 2097152 | tf_op jit(solution)/shard_map/all_to_all | solution.py:212
  16.5 0.1 slice_select_fusion.1
  16.6 8.3 %collective-permute-start.1 = (f32[4,96,256]{2,1,0:T(8,128)S(1)}, f32[4,96,256]{2,1,0:T(8,128)S(1)}, u32[]{:S(2)}, u32[]{:S(2)}) collective-permute-start(f32[4,96,256]{2,1,0:T(8,128)S(1)} %bitcast.36), channel_id=1, source_target_pairs={{0,128},{16,144},{1,129},{17,145},{2,130},{18,146},{3,131},{19,147... | collective-permute-start | bytes 1179656 | tf_op jit(solution)/shard_map/ppermute | solution.py:229
  24.9 7.1 %all-to-all-done = f32[16,64,256]{2,1,0:T(8,128)} async-done(((f32[16,64,256]{2,1,0:T(8,128)}), f32[16,64,256]{2,1,0:T(8,128)}, u32[]{:S(2)}, u32[]{:S(2)}) %all-to-all-start) | async-done | bytes 1048608 | tf_op jit(solution)/shard_map/all_to_all | solution.py:212
  32.0 0.8 slice_bitcast_fusion
  32.9 1.1 broadcast_in_dim.38
  33.9 4.3 %all-to-all-start.1 = ((f32[16,64,256]{2,1,0:T(8,128)}), f32[16,64,256]{2,1,0:T(8,128)S(1)}, u32[]{:S(2)}, u32[]{:S(2)}) async-start(f32[16,64,256]{2,1,0:T(8,128)} %broadcast_in_dim.38), calls=%async_computation.1 | async-start | bytes 2097152 | tf_op jit(solution)/shard_map/all_to_all | solution.py:212
  38.4 4.7 %collective-permute-start.2 = (f32[2,96,256]{2,1,0:T(8,128)S(1)}, f32[2,96,256]{2,1,0:T(8,128)S(1)}, u32[]{:S(2)}, u32[]{:S(2)}) collective-permute-start(f32[2,96,256]{2,1,0:T(8,128)S(1)} %slice.103), channel_id=1, source_target_pairs={{0,64},{16,80},{128,192},{144,208},{1,65},{17,81},{129,193},{145,2... | collective-permute-start | bytes 589832 | tf_op jit(solution)/shard_map/ppermute | solution.py:229
  43.1 2.6 %collective-permute-done.2 = f32[2,96,256]{2,1,0:T(8,128)S(1)} collective-permute-done((f32[2,96,256]{2,1,0:T(8,128)S(1)}, f32[2,96,256]{2,1,0:T(8,128)S(1)}, u32[]{:S(2)}, u32[]{:S(2)}) %collective-permute-start.2) | collective-permute-done | bytes 196640 | tf_op jit(solution)/shard_map/ppermute | solution.py:229
  45.7 1.3 collective-permute-start.3
  47.0 2.2 %collective-permute-done.3 = f32[1,96,256]{2,1,0:T(8,128)S(1)} collective-permute-done((f32[1,96,256]{2,1,0:T(8,128)S(1)}, f32[1,96,256]{2,1,0:T(8,128)S(1)}, u32[]{:S(2)}, u32[]{:S(2)}) %collective-permute-start.3) | collective-permute-done | bytes 98336 | tf_op jit(solution)/shard_map/ppermute | solution.py:229
  49.2 4.0 %all-to-all-done.1 = f32[16,64,256]{2,1,0:T(8,128)S(1)} async-done(((f32[16,64,256]{2,1,0:T(8,128)}), f32[16,64,256]{2,1,0:T(8,128)S(1)}, u32[]{:S(2)}, u32[]{:S(2)}) %all-to-all-start.1) | async-done | bytes 1048608 | tf_op jit(solution)/shard_map/all_to_all | solution.py:212
  53.2 1.8 %fusion.11 = f32[256,256]{1,0:T(8,128)S(1)} fusion(f32[1024,256]{1,0:T(8,128)S(1)} %bitcast.25), kind=kOutput, calls=%fused_computation.32 | convolution fusion | flops 805306368 | bytes 1310720 | tf_op jit(solution)/shard_map/dot_general | solution.py:186
  55.1 3.7 %collective-permute-start.4 = (f32[32,256]{1,0:T(8,128)S(1)}, f32[32,256]{1,0:T(8,128)S(1)}, u32[]{:S(2)}, u32[]{:S(2)}) collective-permute-start(f32[32,256]{1,0:T(8,128)S(1)} %pad_maximum_fusion), channel_id=1, source_target_pairs={{0,16},{16,0},{32,48},{48,32},{64,80},{80,64},{96,112},{112,96},{1... | collective-permute-start | bytes 98312 | tf_op jit(solution)/shard_map/ppermute | solution.py:229
  58.7 0.9 collective-permute-done.4
  59.6 0.7 broadcast_in_dim.40
  60.3 7.8 %all-to-all-start.2 = ((f32[8,32,256]{2,1,0:T(8,128)}), f32[8,32,256]{2,1,0:T(8,128)S(1)}, u32[]{:S(2)}, u32[]{:S(2)}) async-start(f32[8,32,256]{2,1,0:T(8,128)} %broadcast_in_dim.40), calls=%async_computation.2 | async-start | bytes 524288 | tf_op jit(solution)/shard_map/all_to_all | solution.py:212
  68.1 5.1 %fusion.12.products_ref = f32[256,1536]{1,0:T(8,128)S(1)} fusion(f32[1024,256]{1,0:T(8,128)S(1)} %bitcast.27, f32[1024,1536]{1,0:T(8,128)} %param.5), kind=kOutput, calls=%fused_computation.33 | convolution fusion | flops 2415919104 | bytes 8912896 | tf_op jit(solution)/shard_map/dot_general | solution.py:186
  73.3 1.1 slice_select_fusion
  74.3 0.6 collective-permute-start.5
  75.0 4.4 %all-to-all-done.2 = f32[8,32,256]{2,1,0:T(8,128)S(1)} async-done(((f32[8,32,256]{2,1,0:T(8,128)}), f32[8,32,256]{2,1,0:T(8,128)S(1)}, u32[]{:S(2)}, u32[]{:S(2)}) %all-to-all-start.2) | async-done | bytes 262176 | tf_op jit(solution)/shard_map/all_to_all | solution.py:212
  79.4 0.9 broadcast_in_dim.41
  80.3 3.6 %all-to-all-start.3 = ((f32[16,32,256]{2,1,0:T(8,128)}), f32[16,32,256]{2,1,0:T(8,128)S(1)}, u32[]{:S(2)}, u32[]{:S(2)}) async-start(f32[16,32,256]{2,1,0:T(8,128)} %broadcast_in_dim.41), calls=%async_computation.3 | async-start | bytes 1048576 | tf_op jit(solution)/shard_map/all_to_all | solution.py:212
  83.9 2.8 %join.1 = f32[768,256]{1,0:T(8,128)} custom-call(s32[1]{0:T(128)} %bitcast.7.flags, f32[256,1536]{1,0:T(8,128)} %copy-done.1, f32[256,768]{1,0:T(8,128)} %collective-permute-done.5.received_ref), custom_call_target="tpu_custom_call" | custom-call | flops 1000000000 | bytes 4000000 | tf_op jit(solution)/shard_map/join/pallas_call | solution.py:199
  86.7 7.1 %all-to-all-done.3 = f32[16,32,256]{2,1,0:T(8,128)S(1)} async-done(((f32[16,32,256]{2,1,0:T(8,128)}), f32[16,32,256]{2,1,0:T(8,128)S(1)}, u32[]{:S(2)}, u32[]{:S(2)}) %all-to-all-start.3) | async-done | bytes 524320 | tf_op jit(solution)/shard_map/all_to_all | solution.py:212
  93.8 3.5 %all-to-all-start.4 = ((f32[8,96,256]{2,1,0:T(8,128)}), f32[8,96,256]{2,1,0:T(8,128)S(1)}, u32[]{:S(2)}, u32[]{:S(2)}) async-start(f32[8,96,256]{2,1,0:T(8,128)} %bitcast.35), calls=%async_computation.4 | async-start | bytes 1572864 | tf_op jit(solution)/shard_map/all_to_all | solution.py:212
  97.4 0.8 fusion.10
  98.2 14.2 %cholesky.1 = (f32[256,256]{1,0:T(8,128)}, f32[256,256]{1,0:T(8,128)}) custom-call(f32[256,256]{1,0:T(8,128)} %bitcast.38), custom_call_target="tpu_custom_call" | custom-call | flops 14000000000 | bytes 800000 | tf_op jit(solution)/shard_map/cholesky/pallas_call | solution.py:158
  112.4 6.1 %all-to-all-done.4 = f32[8,96,256]{2,1,0:T(8,128)S(1)} async-done(((f32[8,96,256]{2,1,0:T(8,128)}), f32[8,96,256]{2,1,0:T(8,128)S(1)}, u32[]{:S(2)}, u32[]{:S(2)}) %all-to-all-start.4) | async-done | bytes 786464 | tf_op jit(solution)/shard_map/all_to_all | solution.py:212
  118.5 1.2 convolution_add_fusion
  119.8 0.9 broadcast_in_dim.42
  120.7 3.5 %all-to-all-start.5 = ((f32[8,96,256]{2,1,0:T(8,128)}), f32[8,96,256]{2,1,0:T(8,128)S(1)}, u32[]{:S(2)}, u32[]{:S(2)}) async-start(f32[8,96,256]{2,1,0:T(8,128)} %broadcast_in_dim.42), calls=%async_computation.5 | async-start | bytes 1572864 | tf_op jit(solution)/shard_map/all_to_all | solution.py:212
  124.3 6.2 %broadcast_select_fusion = f32[1024,1536]{1,0:T(8,128)} fusion(f32[1024,1536]{1,0:T(8,128)} %param.5, pred[1536]{0:T(1024)(128)(4,1)S(1)} %fusion.6), kind=kLoop, calls=%fused_computation.1 | loop fusion | flops 1572864 | bytes 12584448 | tf_op jit(solution)/shard_map/jit(_where)/select_n | solution.py:264
  130.4 0.7 compare_reduce_fusion
  131.2 13.9 %all-to-all-done.5 = f32[8,96,256]{2,1,0:T(8,128)S(1)} async-done(((f32[8,96,256]{2,1,0:T(8,128)}), f32[8,96,256]{2,1,0:T(8,128)S(1)}, u32[]{:S(2)}, u32[]{:S(2)}) %all-to-all-start.5) | async-done | bytes 786464 | tf_op jit(solution)/shard_map/all_to_all | solution.py:212
  145.1 3.2 %collective-permute-start.6 = (f32[768,256]{1,0:T(8,128)S(1)}, f32[768,256]{1,0:T(8,128)}, u32[]{:S(2)}, u32[]{:S(2)}) collective-permute-start(f32[768,256]{1,0:T(8,128)S(1)} %bitcast.32), channel_id=1, source_target_pairs={{0,16},{16,0},{32,48},{48,32},{64,80},{80,64},{96,112},{112,96},{1... | collective-permute-start | bytes 2359304 | tf_op jit(solution)/shard_map/ppermute | solution.py:229
  148.3 17.0 %lower_upper.1 = (f32[256,256]{1,0:T(8,128)}, f32[2,128,128]{2,1,0:T(8,128)}, f32[256,256]{1,0:T(8,128)}) custom-call(f32[256,256]{1,0:T(8,128)} %bitcast.37, f32[256,256]{1,0:T(8,128)} %get-tuple-element.41.r_ref, f32[256,256]{1,0:T(8,128)} %get-tuple-element.42.inverse_ref), custom_call_target="tpu_custom_call" | custom-call | flops 16999999488 | bytes 1600000 | tf_op jit(solution)/shard_map/lower_upper/pallas_call | solution.py:170
  165.3 1.8 %add_select_fusion = (f32[256,256]{1,0:T(8,128)S(1)}, f32[1024,1536]{1,0:T(8,128)}) fusion(f32[256,256]{1,0:T(8,128)S(1)} %copy-done.3, f32[1024,256]{1,0:T(8,128)S(1)} %bitcast.29, pred[]{:T(512)S(6)} %eq.29, f32[1024,1536]{1,0:T(8,128)} %broadcast_select_fusion, s32[256]{0:T(256)S(1)} %iota_add_fusion, pred[]{:T(512)S(6)} %and.47), kind=kLoop, calls=%fused_computation.10 | loop fusion | flops 589824 | bytes 1311746 | tf_op jit(solution)/shard_map/jit(_where)/select_n | solution.py:275
  167.1 1.6 fusion.13
  168.8 1.9 %fusion.14 = f32[256,768]{1,0:T(8,128)S(1)} fusion(f32[256,256]{1,0:T(8,128)S(1)} %copy-done.2, f32[768,256]{1,0:T(8,128)} %collective-permute-done.6), kind=kOutput, calls=%fused_computation.35 | convolution fusion | flops 301989888 | bytes 1835008 | tf_op jit(solution)/shard_map/dot_general | solution.py:283
  170.7 0.2 maximum_select_fusion
  170.9 0.7 copy-done.4
  171.6 0.7 fusion.3
  172.3 4.6 %convolution_subtract_fusion = f32[1024,1536]{1,0:T(8,128)} fusion(f32[1024,1536]{1,0:T(8,128)S(1)} %copy-done, f32[256,1536]{1,0:T(8,128)S(1)} %fusion.3, f32[768,256]{1,0:T(8,128)S(1)} %slice.97, f32[256,256]{1,0:T(8,128)S(1)} %get-tuple-element.52), kind=kOutput, calls=%fused_computation | convolution fusion | flops 2417754112 | bytes 15204352 | tf_op jit(solution)/shard_map/dot_general | solution.py:182
  (28 shorter events, 0.4 us)
Async XLA Ops:
  5.2 11.2 %collective-permute-start = (f32[768,256]{1,0:T(8,128)S(1)}, f32[768,256]{1,0:T(8,128)S(1)}, u32[]{:S(2)}, u32[]{:S(2)}) collective-permute-start(f32[768,256]{1,0:T(8,128)S(1)} %split.25), channel_id=1, source_target_pairs={{0,16},{1,17},{2,18},{3,19},{4,20},{5,21},{6,22},{7,23},{8,24},{9,... | collective-permute-start | bytes 2359304 | tf_op jit(solution)/shard_map/ppermute | solution.py:229
  8.8 23.2 %all-to-all-start = ((f32[16,64,256]{2,1,0:T(8,128)}), f32[16,64,256]{2,1,0:T(8,128)}, u32[]{:S(2)}, u32[]{:S(2)}) async-start(f32[16,64,256]{2,1,0:T(8,128)} %bitcast), calls=%async_computation | async-start | bytes 2097152 | tf_op jit(solution)/shard_map/all_to_all | solution.py:212
  16.6 21.6 %collective-permute-start.1 = (f32[4,96,256]{2,1,0:T(8,128)S(1)}, f32[4,96,256]{2,1,0:T(8,128)S(1)}, u32[]{:S(2)}, u32[]{:S(2)}) collective-permute-start(f32[4,96,256]{2,1,0:T(8,128)S(1)} %bitcast.36), channel_id=1, source_target_pairs={{0,128},{16,144},{1,129},{17,145},{2,130},{18,146},{3,131},{19,147... | collective-permute-start | bytes 1179656 | tf_op jit(solution)/shard_map/ppermute | solution.py:229
  33.9 19.2 %all-to-all-start.1 = ((f32[16,64,256]{2,1,0:T(8,128)}), f32[16,64,256]{2,1,0:T(8,128)S(1)}, u32[]{:S(2)}, u32[]{:S(2)}) async-start(f32[16,64,256]{2,1,0:T(8,128)} %broadcast_in_dim.38), calls=%async_computation.1 | async-start | bytes 2097152 | tf_op jit(solution)/shard_map/all_to_all | solution.py:212
  38.4 7.3 %collective-permute-start.2 = (f32[2,96,256]{2,1,0:T(8,128)S(1)}, f32[2,96,256]{2,1,0:T(8,128)S(1)}, u32[]{:S(2)}, u32[]{:S(2)}) collective-permute-start(f32[2,96,256]{2,1,0:T(8,128)S(1)} %slice.103), channel_id=1, source_target_pairs={{0,64},{16,80},{128,192},{144,208},{1,65},{17,81},{129,193},{145,2... | collective-permute-start | bytes 589832 | tf_op jit(solution)/shard_map/ppermute | solution.py:229
  45.7 3.5 %collective-permute-start.3 = (f32[1,96,256]{2,1,0:T(8,128)S(1)}, f32[1,96,256]{2,1,0:T(8,128)S(1)}, u32[]{:S(2)}, u32[]{:S(2)}) collective-permute-start(f32[1,96,256]{2,1,0:T(8,128)S(1)} %slice.105), channel_id=1, source_target_pairs={{0,32},{16,48},{64,96},{80,112},{128,160},{144,176},{192,224},{208... | collective-permute-start | bytes 294920 | tf_op jit(solution)/shard_map/ppermute | solution.py:229
  55.1 4.5 %collective-permute-start.4 = (f32[32,256]{1,0:T(8,128)S(1)}, f32[32,256]{1,0:T(8,128)S(1)}, u32[]{:S(2)}, u32[]{:S(2)}) collective-permute-start(f32[32,256]{1,0:T(8,128)S(1)} %pad_maximum_fusion), channel_id=1, source_target_pairs={{0,16},{16,0},{32,48},{48,32},{64,80},{80,64},{96,112},{112,96},{1... | collective-permute-start | bytes 98312 | tf_op jit(solution)/shard_map/ppermute | solution.py:229
  60.3 19.1 %all-to-all-start.2 = ((f32[8,32,256]{2,1,0:T(8,128)}), f32[8,32,256]{2,1,0:T(8,128)S(1)}, u32[]{:S(2)}, u32[]{:S(2)}) async-start(f32[8,32,256]{2,1,0:T(8,128)} %broadcast_in_dim.40), calls=%async_computation.2 | async-start | bytes 524288 | tf_op jit(solution)/shard_map/all_to_all | solution.py:212
  73.3 7.0 %copy-start.1 = (f32[256,1536]{1,0:T(8,128)}, f32[256,1536]{1,0:T(8,128)S(1)}, u32[]{:S(2)}) copy-start(f32[256,1536]{1,0:T(8,128)S(1)} %fusion.12.products_ref) | copy-start | bytes 4718596
  74.3 9.6 %collective-permute-start.5 = (f32[256,768]{1,0:T(8,128)}, f32[256,768]{1,0:T(8,128)}, u32[]{:S(2)}, u32[]{:S(2)}) collective-permute-start(f32[256,768]{1,0:T(8,128)} %slice_select_fusion), channel_id=1, source_target_pairs={{0,16},{16,0},{32,48},{48,32},{64,80},{80,64},{96,112},{112,96},{1... | collective-permute-start | bytes 2359304 | tf_op jit(solution)/shard_map/ppermute | solution.py:229
  80.3 13.5 %all-to-all-start.3 = ((f32[16,32,256]{2,1,0:T(8,128)}), f32[16,32,256]{2,1,0:T(8,128)S(1)}, u32[]{:S(2)}, u32[]{:S(2)}) async-start(f32[16,32,256]{2,1,0:T(8,128)} %broadcast_in_dim.41), calls=%async_computation.3 | async-start | bytes 1048576 | tf_op jit(solution)/shard_map/all_to_all | solution.py:212
  93.8 24.7 %all-to-all-start.4 = ((f32[8,96,256]{2,1,0:T(8,128)}), f32[8,96,256]{2,1,0:T(8,128)S(1)}, u32[]{:S(2)}, u32[]{:S(2)}) async-start(f32[8,96,256]{2,1,0:T(8,128)} %bitcast.35), calls=%async_computation.4 | async-start | bytes 1572864 | tf_op jit(solution)/shard_map/all_to_all | solution.py:212
  120.7 24.4 %all-to-all-start.5 = ((f32[8,96,256]{2,1,0:T(8,128)}), f32[8,96,256]{2,1,0:T(8,128)S(1)}, u32[]{:S(2)}, u32[]{:S(2)}) async-start(f32[8,96,256]{2,1,0:T(8,128)} %broadcast_in_dim.42), calls=%async_computation.5 | async-start | bytes 1572864 | tf_op jit(solution)/shard_map/all_to_all | solution.py:212
  145.1 23.7 %collective-permute-start.6 = (f32[768,256]{1,0:T(8,128)S(1)}, f32[768,256]{1,0:T(8,128)}, u32[]{:S(2)}, u32[]{:S(2)}) collective-permute-start(f32[768,256]{1,0:T(8,128)S(1)} %bitcast.32), channel_id=1, source_target_pairs={{0,16},{16,0},{32,48},{48,32},{64,80},{80,64},{96,112},{112,96},{1... | collective-permute-start | bytes 2359304 | tf_op jit(solution)/shard_map/ppermute | solution.py:229
  148.3 17.0 %copy-start.3 = (f32[256,256]{1,0:T(8,128)S(1)}, f32[256,256]{1,0:T(8,128)}, u32[]{:S(2)}) copy-start(f32[256,256]{1,0:T(8,128)} %get-tuple-element.41.r_ref) | copy-start | bytes 786436
  165.3 3.4 %copy-start.2 = (f32[256,256]{1,0:T(8,128)S(1)}, f32[256,256]{1,0:T(8,128)}, u32[]{:S(2)}) copy-start(f32[256,256]{1,0:T(8,128)} %get-tuple-element.43) | copy-start | bytes 786436
  167.1 5.2 %copy-start = (f32[1024,1536]{1,0:T(8,128)S(1)}, f32[1024,1536]{1,0:T(8,128)}, u32[]{:S(2)}) copy-start(f32[1024,1536]{1,0:T(8,128)} %get-tuple-element.53) | copy-start | bytes 18874372
  170.7 1.0 copy-start.4

commit v3 on v2

--- a/solution.py
+++ b/solution.py
@@ -223,7 +223,7 @@
     on_top, has_panel = my_row == 0, my_col == 0
     levels = [[CORES * z + c for z in range(LEVELS)] for c in range(CORES)]
     rows, cols = matrix.shape
-    high = lax.Precision.HIGH
+    high, highest = lax.Precision.HIGH, lax.Precision.HIGHEST
 
     def permute(value, pairs):
         return lax.ppermute(value, "prow", pairs)
@@ -257,7 +257,7 @@
     squares = jnp.concatenate([squares[0], jnp.where(on_top, squares[1], 0.0)], axis=0)
     squares, panel = lax.optimization_barrier((squares + swap(squares), panel))
     squares = gather(squares, "prow", LEVELS, levels)
-    products = transposed_product(panel, matrix, high)
+    products = transposed_product(panel, matrix)
     low_half, high_half = jnp.split(products, CORES, axis=1)
     other = jnp.where(core == 0, high_half, low_half)
     squares = gather(squares.sum(0), "pcol", cols_count)
@@ -281,7 +281,7 @@
     sibling = swap(summed)
     mine, other = (
         lax.dot_general(
-            square, a, (((1,), (1,)), ((), ())), precision=high, preferred_element_type=f32
+            square, a, (((1,), (1,)), ((), ())), precision=highest, preferred_element_type=f32
         )
         for a in (summed, sibling)
     )

time: 178 us -> 183 us (1.028)
  matrix products: 16.3 us -> 19.1 us
  waiting for transfers between devices: 48.2 us -> 50.9 us
    ppermute x7, starting transfers between devices: 23 us -> 20.3 us  [permute(): return lax.ppermute(value, 'prow', pairs)]
    all_to_all x6, waiting for transfers between devices: 42.6 us -> 45.2 us  [exchange(): return lax.all_to_all(pieces, axis, 0, 0, axis_index_groups=groups)]
    all_to_all x6, starting transfers between devices: 30.5 us -> 33.1 us  [exchange(): return lax.all_to_all(pieces, axis, 0, 0, axis_index_groups=groups)]
    dot_general x2, matrix products: 6.94 us -> 9.4 us  [transposed_product(): lax.dot_general(left, right, (((0,), (0,)), ((), ())), precision=precisio...]
  transfers between devices with their start and end apart: 13 -> 13, of which waited for: 9 -> 9; matrix products, arithmetic and copies ran while one was open for 13% -> 14% of each run, Pallas kernels for 19% -> 19%
where the time goes in v3:
time: 183 us; the launch traced here: 182 us
  starting transfers between devices  53.4 us (29%)
  waiting for transfers between devices  50.9 us (28%)
  Pallas kernels  34 us (19%)
  matrix products  19.1 us (10%)
  local copies, waits for them, and re-layouts  13 us (7%)
  other arithmetic  10.9 us (6%)
    all_to_all x6, waiting for transfers between devices, exchange(): return lax.all_to_all(pieces, axis, 0, 0, axis_index_groups=groups)  45.2 us
    all_to_all x6, starting transfers between devices, exchange(): return lax.all_to_all(pieces, axis, 0, 0, axis_index_groups=groups)  33.1 us
    ppermute x7, starting transfers between devices, permute(): return lax.ppermute(value, 'prow', pairs)  20.3 us
    pallas_call x1, Pallas kernels, lower_upper(): pl.pallas_call(lower_upper_kernel, out_shape=(square_shape, jax.ShapeDtyp...  17 us
    pallas_call x1, Pallas kernels, cholesky(): pl.pallas_call(cholesky_kernel, out_shape=(square_shape,) * 2, scratch_sh...  14.2 us
    dot_general x2, matrix products, transposed_product(): lax.dot_general(left, right, (((0,), (0,)), ((), ())), precision=precisio...  9.4 us
    select_n x1, other arithmetic, per_device(): base = lax.optimization_barrier(jnp.where(replaced, 0.0, matrix))  6.16 us
    dot_general x2, matrix products, product(): return jnp.dot(left, right, precision=precision, preferred_element_type=f32)  5.84 us
  transfers between devices with their start and end apart: 13, of which 9 were waited for; matrix products, arithmetic and copies ran while one was open for 14% of the time, Pallas kernels for 19%

profile of v3, /device:TPU:1, one launch (start us, length us, event | category | flops | bytes accessed | tf_op | source)
XLA Modules:
  0.0 182.3 jit_solution(5057854702426650392)
XLA Ops:
  0.6 2.7 %slice.86 = f32[256,1536]{1,0:T(8,128)} slice(f32[1024,1536]{1,0:T(8,128)} %param.5), slice={[0:256], [0:1536]} | slice | bytes 3145728 | tf_op jit(solution)/shard_map/slice | solution.py:238
  3.3 1.9 %copy.5 = f32[256,1536]{0,1:T(8,128)S(1)} copy(f32[256,1536]{1,0:T(8,128)} %slice.86) | data formatting | bytes 3145728
  5.2 1.3 collective-permute-start
  6.5 2.3 %slice.84 = f32[1024,256]{1,0:T(8,128)} slice(f32[1024,1536]{1,0:T(8,128)} %param.5), slice={[0:1024], [0:256]} | slice | bytes 2097152 | tf_op jit(solution)/shard_map/slice | solution.py:236
  8.8 7.6 %all-to-all-start = ((f32[16,64,256]{2,1,0:T(8,128)}), f32[16,64,256]{2,1,0:T(8,128)}, u32[]{:S(2)}, u32[]{:S(2)}) async-start(f32[16,64,256]{2,1,0:T(8,128)} %bitcast), calls=%async_computation | async-start | bytes 2097152 | tf_op jit(solution)/shard_map/all_to_all | solution.py:212
  16.5 0.1 slice_select_fusion.1
  16.6 8.3 %collective-permute-start.1 = (f32[4,96,256]{2,1,0:T(8,128)S(1)}, f32[4,96,256]{2,1,0:T(8,128)S(1)}, u32[]{:S(2)}, u32[]{:S(2)}) collective-permute-start(f32[4,96,256]{2,1,0:T(8,128)S(1)} %bitcast.36), channel_id=1, source_target_pairs={{0,128},{16,144},{1,129},{17,145},{2,130},{18,146},{3,131},{19,147... | collective-permute-start | bytes 1179656 | tf_op jit(solution)/shard_map/ppermute | solution.py:229
  24.9 7.1 %all-to-all-done = f32[16,64,256]{2,1,0:T(8,128)} async-done(((f32[16,64,256]{2,1,0:T(8,128)}), f32[16,64,256]{2,1,0:T(8,128)}, u32[]{:S(2)}, u32[]{:S(2)}) %all-to-all-start) | async-done | bytes 1048608 | tf_op jit(solution)/shard_map/all_to_all | solution.py:212
  32.0 0.8 slice_bitcast_fusion
  32.9 1.1 broadcast_in_dim.38
  33.9 4.3 %all-to-all-start.1 = ((f32[16,64,256]{2,1,0:T(8,128)}), f32[16,64,256]{2,1,0:T(8,128)S(1)}, u32[]{:S(2)}, u32[]{:S(2)}) async-start(f32[16,64,256]{2,1,0:T(8,128)} %broadcast_in_dim.38), calls=%async_computation.1 | async-start | bytes 2097152 | tf_op jit(solution)/shard_map/all_to_all | solution.py:212
  38.4 4.7 %collective-permute-start.2 = (f32[2,96,256]{2,1,0:T(8,128)S(1)}, f32[2,96,256]{2,1,0:T(8,128)S(1)}, u32[]{:S(2)}, u32[]{:S(2)}) collective-permute-start(f32[2,96,256]{2,1,0:T(8,128)S(1)} %slice.103), channel_id=1, source_target_pairs={{0,64},{16,80},{128,192},{144,208},{1,65},{17,81},{129,193},{145,2... | collective-permute-start | bytes 589832 | tf_op jit(solution)/shard_map/ppermute | solution.py:229
  43.1 2.6 %collective-permute-done.2 = f32[2,96,256]{2,1,0:T(8,128)S(1)} collective-permute-done((f32[2,96,256]{2,1,0:T(8,128)S(1)}, f32[2,96,256]{2,1,0:T(8,128)S(1)}, u32[]{:S(2)}, u32[]{:S(2)}) %collective-permute-start.2) | collective-permute-done | bytes 196640 | tf_op jit(solution)/shard_map/ppermute | solution.py:229
  45.7 1.3 collective-permute-start.3
  47.0 2.2 %collective-permute-done.3 = f32[1,96,256]{2,1,0:T(8,128)S(1)} collective-permute-done((f32[1,96,256]{2,1,0:T(8,128)S(1)}, f32[1,96,256]{2,1,0:T(8,128)S(1)}, u32[]{:S(2)}, u32[]{:S(2)}) %collective-permute-start.3) | collective-permute-done | bytes 98336 | tf_op jit(solution)/shard_map/ppermute | solution.py:229
  49.2 4.0 %all-to-all-done.1 = f32[16,64,256]{2,1,0:T(8,128)S(1)} async-done(((f32[16,64,256]{2,1,0:T(8,128)}), f32[16,64,256]{2,1,0:T(8,128)S(1)}, u32[]{:S(2)}, u32[]{:S(2)}) %all-to-all-start.1) | async-done | bytes 1048608 | tf_op jit(solution)/shard_map/all_to_all | solution.py:212
  53.2 1.8 %fusion.11 = f32[256,256]{1,0:T(8,128)S(1)} fusion(f32[1024,256]{1,0:T(8,128)S(1)} %bitcast.25), kind=kOutput, calls=%fused_computation.32 | convolution fusion | flops 805306368 | bytes 1310720 | tf_op jit(solution)/shard_map/dot_general | solution.py:186
  55.1 3.7 %collective-permute-start.4 = (f32[32,256]{1,0:T(8,128)S(1)}, f32[32,256]{1,0:T(8,128)S(1)}, u32[]{:S(2)}, u32[]{:S(2)}) collective-permute-start(f32[32,256]{1,0:T(8,128)S(1)} %pad_maximum_fusion), channel_id=1, source_target_pairs={{0,16},{16,0},{32,48},{48,32},{64,80},{80,64},{96,112},{112,96},{1... | collective-permute-start | bytes 98312 | tf_op jit(solution)/shard_map/ppermute | solution.py:229
  58.7 0.9 collective-permute-done.4
  59.6 0.7 broadcast_in_dim.40
  60.3 7.8 %all-to-all-start.2 = ((f32[8,32,256]{2,1,0:T(8,128)}), f32[8,32,256]{2,1,0:T(8,128)S(1)}, u32[]{:S(2)}, u32[]{:S(2)}) async-start(f32[8,32,256]{2,1,0:T(8,128)} %broadcast_in_dim.40), calls=%async_computation.2 | async-start | bytes 524288 | tf_op jit(solution)/shard_map/all_to_all | solution.py:212
  68.1 7.6 %fusion.12.products_ref = f32[256,1536]{1,0:T(8,128)S(1)} fusion(f32[1024,256]{1,0:T(8,128)S(1)} %bitcast.27, f32[1024,1536]{1,0:T(8,128)} %param.5), kind=kOutput, calls=%fused_computation.33 | convolution fusion | flops 4831838208 | bytes 8912896 | tf_op jit(solution)/shard_map/dot_general | solution.py:186
  75.7 1.1 slice_select_fusion
  76.8 0.6 collective-permute-start.5
  77.4 1.9 %all-to-all-done.2 = f32[8,32,256]{2,1,0:T(8,128)S(1)} async-done(((f32[8,32,256]{2,1,0:T(8,128)}), f32[8,32,256]{2,1,0:T(8,128)S(1)}, u32[]{:S(2)}, u32[]{:S(2)}) %all-to-all-start.2) | async-done | bytes 262176 | tf_op jit(solution)/shard_map/all_to_all | solution.py:212
  79.4 0.9 broadcast_in_dim.41
  80.3 3.6 %all-to-all-start.3 = ((f32[16,32,256]{2,1,0:T(8,128)}), f32[16,32,256]{2,1,0:T(8,128)S(1)}, u32[]{:S(2)}, u32[]{:S(2)}) async-start(f32[16,32,256]{2,1,0:T(8,128)} %broadcast_in_dim.41), calls=%async_computation.3 | async-start | bytes 1048576 | tf_op jit(solution)/shard_map/all_to_all | solution.py:212
  83.9 2.8 %join.1 = f32[768,256]{1,0:T(8,128)} custom-call(s32[1]{0:T(128)} %bitcast.7.flags, f32[256,1536]{1,0:T(8,128)} %copy-done.1, f32[256,768]{1,0:T(8,128)} %collective-permute-done.5.received_ref), custom_call_target="tpu_custom_call" | custom-call | flops 1000000000 | bytes 4000000 | tf_op jit(solution)/shard_map/join/pallas_call | solution.py:199
  86.7 7.1 %all-to-all-done.3 = f32[16,32,256]{2,1,0:T(8,128)S(1)} async-done(((f32[16,32,256]{2,1,0:T(8,128)}), f32[16,32,256]{2,1,0:T(8,128)S(1)}, u32[]{:S(2)}, u32[]{:S(2)}) %all-to-all-start.3) | async-done | bytes 524320 | tf_op jit(solution)/shard_map/all_to_all | solution.py:212
  93.8 6.1 %all-to-all-start.4 = ((f32[8,96,256]{2,1,0:T(8,128)}), f32[8,96,256]{2,1,0:T(8,128)S(1)}, u32[]{:S(2)}, u32[]{:S(2)}) async-start(f32[8,96,256]{2,1,0:T(8,128)} %bitcast.35), calls=%async_computation.4 | async-start | bytes 1572864 | tf_op jit(solution)/shard_map/all_to_all | solution.py:212
  99.9 0.8 fusion.10
  100.8 14.2 %cholesky.1 = (f32[256,256]{1,0:T(8,128)}, f32[256,256]{1,0:T(8,128)}) custom-call(f32[256,256]{1,0:T(8,128)} %bitcast.38), custom_call_target="tpu_custom_call" | custom-call | flops 14000000000 | bytes 800000 | tf_op jit(solution)/shard_map/cholesky/pallas_call | solution.py:158
  114.9 8.6 %all-to-all-done.4 = f32[8,96,256]{2,1,0:T(8,128)S(1)} async-done(((f32[8,96,256]{2,1,0:T(8,128)}), f32[8,96,256]{2,1,0:T(8,128)S(1)}, u32[]{:S(2)}, u32[]{:S(2)}) %all-to-all-start.4) | async-done | bytes 786464 | tf_op jit(solution)/shard_map/all_to_all | solution.py:212
  123.6 1.2 convolution_add_fusion
  124.8 0.9 broadcast_in_dim.42
  125.7 3.5 %all-to-all-start.5 = ((f32[8,96,256]{2,1,0:T(8,128)}), f32[8,96,256]{2,1,0:T(8,128)S(1)}, u32[]{:S(2)}, u32[]{:S(2)}) async-start(f32[8,96,256]{2,1,0:T(8,128)} %broadcast_in_dim.42), calls=%async_computation.5 | async-start | bytes 1572864 | tf_op jit(solution)/shard_map/all_to_all | solution.py:212
  129.3 6.2 %broadcast_select_fusion = f32[1024,1536]{1,0:T(8,128)} fusion(f32[1024,1536]{1,0:T(8,128)} %param.5, pred[1536]{0:T(1024)(128)(4,1)S(1)} %fusion.6), kind=kLoop, calls=%fused_computation.1 | loop fusion | flops 1572864 | bytes 12584448 | tf_op jit(solution)/shard_map/jit(_where)/select_n | solution.py:264
  135.5 0.7 compare_reduce_fusion
  136.2 16.6 %all-to-all-done.5 = f32[8,96,256]{2,1,0:T(8,128)S(1)} async-done(((f32[8,96,256]{2,1,0:T(8,128)}), f32[8,96,256]{2,1,0:T(8,128)S(1)}, u32[]{:S(2)}, u32[]{:S(2)}) %all-to-all-start.5) | async-done | bytes 786464 | tf_op jit(solution)/shard_map/all_to_all | solution.py:212
  152.8 0.5 collective-permute-start.6
  153.3 17.0 %lower_upper.1 = (f32[256,256]{1,0:T(8,128)}, f32[2,128,128]{2,1,0:T(8,128)}, f32[256,256]{1,0:T(8,128)}) custom-call(f32[256,256]{1,0:T(8,128)} %bitcast.37, f32[256,256]{1,0:T(8,128)} %get-tuple-element.41.r_ref, f32[256,256]{1,0:T(8,128)} %get-tuple-element.42.inverse_ref), custom_call_target="tpu_custom_call" | custom-call | flops 16999999488 | bytes 1600000 | tf_op jit(solution)/shard_map/lower_upper/pallas_call | solution.py:170
  170.3 1.8 add_select_fusion
  172.1 1.9 %fusion.13 = f32[256,768]{1,0:T(8,128)S(1)} fusion(f32[256,256]{1,0:T(8,128)} %get-tuple-element.43, f32[768,256]{1,0:T(8,128)S(1)} %bitcast.33), kind=kOutput, calls=%fused_computation.34 | convolution fusion | flops 603979776 | bytes 1835008 | tf_op jit(solution)/shard_map/dot_general | solution.py:283
  174.0 2.0 %fusion.14 = f32[256,768]{1,0:T(8,128)S(1)} fusion(f32[256,256]{1,0:T(8,128)S(1)} %copy-done.2, f32[768,256]{1,0:T(8,128)} %collective-permute-done.6), kind=kOutput, calls=%fused_computation.35 | convolution fusion | flops 603979776 | bytes 1835008 | tf_op jit(solution)/shard_map/dot_general | solution.py:283
  176.0 0.2 maximum_select_fusion
  176.2 0.7 copy-done.4
  177.0 0.7 fusion.3
  177.7 4.6 %convolution_subtract_fusion = f32[1024,1536]{1,0:T(8,128)} fusion(f32[1024,1536]{1,0:T(8,128)S(1)} %copy-done, f32[256,1536]{1,0:T(8,128)S(1)} %fusion.3, f32[768,256]{1,0:T(8,128)S(1)} %slice.97, f32[256,256]{1,0:T(8,128)S(1)} %get-tuple-element.52), kind=kOutput, calls=%fused_computation | convolution fusion | flops 2417754112 | bytes 15204352 | tf_op jit(solution)/shard_map/dot_general | solution.py:182
  (28 shorter events, 0.4 us)
Async XLA Ops:
  5.2 11.2 %collective-permute-start = (f32[768,256]{1,0:T(8,128)S(1)}, f32[768,256]{1,0:T(8,128)S(1)}, u32[]{:S(2)}, u32[]{:S(2)}) collective-permute-start(f32[768,256]{1,0:T(8,128)S(1)} %split.25), channel_id=1, source_target_pairs={{0,16},{1,17},{2,18},{3,19},{4,20},{5,21},{6,22},{7,23},{8,24},{9,... | collective-permute-start | bytes 2359304 | tf_op jit(solution)/shard_map/ppermute | solution.py:229
  8.8 23.2 %all-to-all-start = ((f32[16,64,256]{2,1,0:T(8,128)}), f32[16,64,256]{2,1,0:T(8,128)}, u32[]{:S(2)}, u32[]{:S(2)}) async-start(f32[16,64,256]{2,1,0:T(8,128)} %bitcast), calls=%async_computation | async-start | bytes 2097152 | tf_op jit(solution)/shard_map/all_to_all | solution.py:212
  16.6 21.6 %collective-permute-start.1 = (f32[4,96,256]{2,1,0:T(8,128)S(1)}, f32[4,96,256]{2,1,0:T(8,128)S(1)}, u32[]{:S(2)}, u32[]{:S(2)}) collective-permute-start(f32[4,96,256]{2,1,0:T(8,128)S(1)} %bitcast.36), channel_id=1, source_target_pairs={{0,128},{16,144},{1,129},{17,145},{2,130},{18,146},{3,131},{19,147... | collective-permute-start | bytes 1179656 | tf_op jit(solution)/shard_map/ppermute | solution.py:229
  33.9 19.2 %all-to-all-start.1 = ((f32[16,64,256]{2,1,0:T(8,128)}), f32[16,64,256]{2,1,0:T(8,128)S(1)}, u32[]{:S(2)}, u32[]{:S(2)}) async-start(f32[16,64,256]{2,1,0:T(8,128)} %broadcast_in_dim.38), calls=%async_computation.1 | async-start | bytes 2097152 | tf_op jit(solution)/shard_map/all_to_all | solution.py:212
  38.4 7.3 %collective-permute-start.2 = (f32[2,96,256]{2,1,0:T(8,128)S(1)}, f32[2,96,256]{2,1,0:T(8,128)S(1)}, u32[]{:S(2)}, u32[]{:S(2)}) collective-permute-start(f32[2,96,256]{2,1,0:T(8,128)S(1)} %slice.103), channel_id=1, source_target_pairs={{0,64},{16,80},{128,192},{144,208},{1,65},{17,81},{129,193},{145,2... | collective-permute-start | bytes 589832 | tf_op jit(solution)/shard_map/ppermute | solution.py:229
  45.7 3.5 %collective-permute-start.3 = (f32[1,96,256]{2,1,0:T(8,128)S(1)}, f32[1,96,256]{2,1,0:T(8,128)S(1)}, u32[]{:S(2)}, u32[]{:S(2)}) collective-permute-start(f32[1,96,256]{2,1,0:T(8,128)S(1)} %slice.105), channel_id=1, source_target_pairs={{0,32},{16,48},{64,96},{80,112},{128,160},{144,176},{192,224},{208... | collective-permute-start | bytes 294920 | tf_op jit(solution)/shard_map/ppermute | solution.py:229
  55.1 4.5 %collective-permute-start.4 = (f32[32,256]{1,0:T(8,128)S(1)}, f32[32,256]{1,0:T(8,128)S(1)}, u32[]{:S(2)}, u32[]{:S(2)}) collective-permute-start(f32[32,256]{1,0:T(8,128)S(1)} %pad_maximum_fusion), channel_id=1, source_target_pairs={{0,16},{16,0},{32,48},{48,32},{64,80},{80,64},{96,112},{112,96},{1... | collective-permute-start | bytes 98312 | tf_op jit(solution)/shard_map/ppermute | solution.py:229
  60.3 19.1 %all-to-all-start.2 = ((f32[8,32,256]{2,1,0:T(8,128)}), f32[8,32,256]{2,1,0:T(8,128)S(1)}, u32[]{:S(2)}, u32[]{:S(2)}) async-start(f32[8,32,256]{2,1,0:T(8,128)} %broadcast_in_dim.40), calls=%async_computation.2 | async-start | bytes 524288 | tf_op jit(solution)/shard_map/all_to_all | solution.py:212
  75.7 4.5 %copy-start.1 = (f32[256,1536]{1,0:T(8,128)}, f32[256,1536]{1,0:T(8,128)S(1)}, u32[]{:S(2)}) copy-start(f32[256,1536]{1,0:T(8,128)S(1)} %fusion.12.products_ref) | copy-start | bytes 4718596
  76.8 7.1 %collective-permute-start.5 = (f32[256,768]{1,0:T(8,128)}, f32[256,768]{1,0:T(8,128)}, u32[]{:S(2)}, u32[]{:S(2)}) collective-permute-start(f32[256,768]{1,0:T(8,128)} %slice_select_fusion), channel_id=1, source_target_pairs={{0,16},{16,0},{32,48},{48,32},{64,80},{80,64},{96,112},{112,96},{1... | collective-permute-start | bytes 2359304 | tf_op jit(solution)/shard_map/ppermute | solution.py:229
  80.3 13.5 %all-to-all-start.3 = ((f32[16,32,256]{2,1,0:T(8,128)}), f32[16,32,256]{2,1,0:T(8,128)S(1)}, u32[]{:S(2)}, u32[]{:S(2)}) async-start(f32[16,32,256]{2,1,0:T(8,128)} %broadcast_in_dim.41), calls=%async_computation.3 | async-start | bytes 1048576 | tf_op jit(solution)/shard_map/all_to_all | solution.py:212
  93.8 29.7 %all-to-all-start.4 = ((f32[8,96,256]{2,1,0:T(8,128)}), f32[8,96,256]{2,1,0:T(8,128)S(1)}, u32[]{:S(2)}, u32[]{:S(2)}) async-start(f32[8,96,256]{2,1,0:T(8,128)} %bitcast.35), calls=%async_computation.4 | async-start | bytes 1572864 | tf_op jit(solution)/shard_map/all_to_all | solution.py:212
  125.7 27.0 %all-to-all-start.5 = ((f32[8,96,256]{2,1,0:T(8,128)}), f32[8,96,256]{2,1,0:T(8,128)S(1)}, u32[]{:S(2)}, u32[]{:S(2)}) async-start(f32[8,96,256]{2,1,0:T(8,128)} %broadcast_in_dim.42), calls=%async_computation.5 | async-start | bytes 1572864 | tf_op jit(solution)/shard_map/all_to_all | solution.py:212
  152.8 21.3 %collective-permute-start.6 = (f32[768,256]{1,0:T(8,128)S(1)}, f32[768,256]{1,0:T(8,128)}, u32[]{:S(2)}, u32[]{:S(2)}) collective-permute-start(f32[768,256]{1,0:T(8,128)S(1)} %bitcast.32), channel_id=1, source_target_pairs={{0,16},{16,0},{32,48},{48,32},{64,80},{80,64},{96,112},{112,96},{1... | collective-permute-start | bytes 2359304 | tf_op jit(solution)/shard_map/ppermute | solution.py:229
  153.3 17.0 %copy-start.3 = (f32[256,256]{1,0:T(8,128)S(1)}, f32[256,256]{1,0:T(8,128)}, u32[]{:S(2)}) copy-start(f32[256,256]{1,0:T(8,128)} %get-tuple-element.41.r_ref) | copy-start | bytes 786436
  170.3 3.7 %copy-start.2 = (f32[256,256]{1,0:T(8,128)S(1)}, f32[256,256]{1,0:T(8,128)}, u32[]{:S(2)}) copy-start(f32[256,256]{1,0:T(8,128)} %get-tuple-element.43) | copy-start | bytes 786436
  172.1 5.6 %copy-start = (f32[1024,1536]{1,0:T(8,128)S(1)}, f32[1024,1536]{1,0:T(8,128)}, u32[]{:S(2)}) copy-start(f32[1024,1536]{1,0:T(8,128)} %get-tuple-element.53) | copy-start | bytes 18874372
  176.0 1.0 copy-start.4
